TPU v7x, 256 devices: a whole 4x4x8 slice. The times are simulated.
256 devices in a mesh: cand: 2 (over core), mp: 64 (over y, x_lo, z), dp: 2 (over x_hi).
Axes of the slice: x: 4 (x_hi: 2, x_lo: 2; x = x_hi * 2 + x_lo), y: 4, z: 8, core: 2. Of those that a mesh axis runs over, the one named last changes fastest.
Arguments:
- clean: bfloat16 [1536, 768], P('mp', 'dp'), may hold values from -3 to 3
- noise: bfloat16 [1536, 768], P('mp', 'dp'), may hold values from -6 to 6
- level_index: int32 [12], P('dp'), may hold values from 0 to 31
- snap_first: bfloat16 [16, 9, 1536, 1536], P('cand', None, 'mp'), may hold values from -0.0546875 to 0.0546875
- snap_second: bfloat16 [16, 9, 1536, 1536], P('cand', None, 'mp'), may hold values from -0.0546875 to 0.0546875
- blend: float32 [4, 8], P('cand'), may hold values from -1.4 to 1.4
- snap_index: int32 [4, 8], P('cand'), may hold values from 0 to 15
Outputs:
- losses: float32 [4], P('cand')
- denoised: bfloat16 [4, 1536, 768], P('cand', 'mp', 'dp')
All inputs are finite; a program needn't handle non-finite values.
Results may differ from a plain program's by a relative error of at most 0.00265.
The roundings to bfloat16 on the way count: a program that leaves them out, or rounds other values in their place, can miss the bound.
Values may be sent and summed in bfloat16 or wider, within the bound.
No kernel may reach another device: no remote copies, remote signals or barrier semaphores. Data moves between devices by JAX's collectives and lax.ppermute only.
A program may use at most 128 MiB of HBM per device.

v0:
```python
import jax
import jax.numpy as jnp
from jax import lax
from jax.sharding import Mesh
from jax.sharding import PartitionSpec as P

LEVELS = 32
MP = ("mp_0", "mp_1", "mp_2")


SIGMA_DATA = 0.5


def sent_to_all(value, axis):
    copies = jnp.broadcast_to(value, (lax.axis_size(axis), *value.shape))
    return lax.all_to_all(copies, axis, split_axis=0, concat_axis=0, tiled=True)


def joined_along(pieces, dim):
    pieces = jnp.moveaxis(pieces, 0, dim)
    lengths = pieces.shape
    return pieces.reshape(*lengths[:dim], lengths[dim] * lengths[dim + 1], *lengths[dim + 2 :])


def gathered_copies(value, axis, dim):
    pieces = sent_to_all(value, axis)
    return joined_along(pieces, dim)


def from_partner(value, axis, apart):
    return lax.ppermute(value, axis, [(i, i ^ 1 << apart) for i in range(lax.axis_size(axis))])


def split_up(value, dim, size):
    lengths = value.shape
    pieces = value.reshape(*lengths[:dim], size, lengths[dim] // size, *lengths[dim + 1 :])
    return jnp.moveaxis(pieces, dim, 0)


def sum_at_owner(value, axis, dim):
    pieces = split_up(value, dim, lax.axis_size(axis))
    arrived = lax.all_to_all(pieces, axis, split_axis=0, concat_axis=0, tiled=True)
    return arrived.sum(axis=0)


def summed_rows(value, axes, dim):
    far, near = axes
    initial = sum_at_owner(value, far, dim)
    return sum_at_owner(initial, near, dim)


def over_copies(value, axis):
    return sent_to_all(value, axis).sum(axis=0)


def over_axes(value, axes):
    far, near = axes
    return over_copies(over_copies(value, near), far)


def noise_scale(level_index):
    ratio = 2.0 * level_index.astype(jnp.float32) / (LEVELS - 1) - 1.0
    return jnp.exp(-0.4 + 2.0 * ratio)


def tap_shift(values, down_by, right_by):
    length_all = values.shape[-1]
    offset = down_by * 8 + right_by
    padded = jnp.pad(values, [(0, 0)] * (values.ndim - 1) + [(9, 9)])
    moved = lax.slice_in_dim(padded, 9 + offset, 9 + offset + length_all, axis=values.ndim - 1)
    within = jnp.arange(length_all) % 64
    map_row = within // 8
    map_col = within % 8
    inside = (
        (map_row + down_by >= 0)
        & (map_row + down_by < 8)
        & (map_col + right_by >= 0)
        & (map_col + right_by < 8)
    )
    return jnp.where(inside, moved, jnp.zeros_like(moved))


def tap_stack(values):
    return jnp.stack(
        [tap_shift(values, down_by, right_by) for down_by in (-1, 0, 1) for right_by in (-1, 0, 1)],
        0,
    )


def blend_owned(first_own, second_own, mixing, first_slot):
    members = mixing.shape[0]
    shape = (members,) + first_own.shape[1:]

    def accumulate(which, totals):
        coeff = lax.dynamic_slice_in_dim(mixing, first_slot + which, 1, 1)[:, 0][
            :, None, None, None
        ]
        first_snap = lax.dynamic_index_in_dim(first_own, which, 0, keepdims=False).astype(
            jnp.float32
        )
        second_snap = lax.dynamic_index_in_dim(second_own, which, 0, keepdims=False).astype(
            jnp.float32
        )
        return (totals[0] + coeff * first_snap[None], totals[1] + coeff * second_snap[None])

    empty = jnp.zeros(shape, jnp.float32)
    return lax.fori_loop(0, first_own.shape[0], accumulate, (empty, empty))


def on_device(clean, noise, level_index, snap_first, snap_second, blend, snap_index):
    sigmas = jnp.repeat(noise_scale(level_index), 64)
    spread = sigmas * sigmas + SIGMA_DATA * SIGMA_DATA
    scale_in = 1.0 / jnp.sqrt(spread)
    scale_skip = SIGMA_DATA * SIGMA_DATA / spread
    scale_out = sigmas * SIGMA_DATA / jnp.sqrt(spread)
    weighting = spread / (sigmas * SIGMA_DATA) ** 2
    clean_f = clean.astype(jnp.float32)
    noisy = clean_f + sigmas * noise.astype(jnp.float32)
    x_own = (scale_in * noisy).astype(jnp.bfloat16)
    x_full = gathered_copies(x_own, MP, 0)
    x_stack = tap_stack(x_full)
    owned = snap_first.shape[0]
    stored = owned * lax.axis_size("cand")
    onehot = (snap_index[:, :, None] == jnp.arange(stored, dtype=jnp.int32)[None, None, :]).astype(
        jnp.float32
    )
    mixing = jnp.sum(blend[:, :, None] * onehot, 1)
    first_slot = lax.axis_index("cand") * owned
    other_mix = from_partner(mixing, "cand", 0)
    mine_first, mine_second = blend_owned(snap_first, snap_second, mixing, first_slot)
    give_first, give_second = blend_owned(snap_first, snap_second, other_mix, first_slot)
    got_first, got_second = from_partner((give_first, give_second), "cand", 0)
    first_w = (mine_first + got_first).astype(jnp.bfloat16)
    second_w = (mine_second + got_second).astype(jnp.bfloat16)
    preact = jnp.einsum("gkoc,kct->got", first_w, x_stack, preferred_element_type=jnp.float32)
    hidden = jax.nn.silu(preact).astype(jnp.bfloat16)
    h_stack = tap_stack(hidden)
    shares = summed_rows(
        jnp.einsum("gkio,kgit->ogt", second_w, h_stack, preferred_element_type=jnp.float32),
        ("mp_0", ("mp_1", "mp_2")),
        0,
    )
    features = jnp.transpose(shares, (1, 0, 2))
    denoised_f = scale_skip[None, None, :] * noisy[None] + scale_out[None, None, :] * features
    partial_value = jnp.sum(
        weighting[None, None, :] * (denoised_f - clean_f[None]) ** 2, axis=(1, 2)
    )
    entries = clean.shape[0] * lax.axis_size(MP) * clean.shape[1] * lax.axis_size("dp")
    totals = over_axes(partial_value, (("mp_0", "mp_1"), ("mp_2", "dp")))
    losses = totals / entries
    return (losses, denoised_f.astype(jnp.bfloat16))


def solution(mesh):
    torus = Mesh(
        mesh.devices.reshape(mesh.shape["cand"], 4, 2, 8, mesh.shape["dp"]),
        ("cand", "mp_0", "mp_1", "mp_2", "dp"),
    )
    return jax.shard_map(
        on_device,
        mesh=torus,
        in_specs=(
            P(MP, "dp"),
            P(MP, "dp"),
            P("dp"),
            P("cand", None, MP, None),
            P("cand", None, MP, None),
            P("cand", None),
            P("cand", None),
        ),
        out_specs=(P("cand"), P("cand", MP, "dp")),
        check_vma=False,
    )
```

profile of v0, /device:TPU:8, one launch (start us, length us, event | category | flops | bytes accessed | tf_op | source)
XLA Modules:
  0.0 283.6 jit_solution(17623462076799888759)
XLA Ops:
  3.4 13.2 %all-to-all-start = ((bf16[64,24,384]{2,1,0:T(8,128)(2,1)}), bf16[64,24,384]{2,1,0:T(8,128)(2,1)}, u32[]{:S(2)}, u32[]{:S(2)}) async-start(bf16[64,24,384]{2,1,0:T(8,128)(2,1)} %broadcast_in_dim.92), calls=%async_computation | async-start | bytes 2359296 | tf_op jit(solution)/shard_map/all_to_all | solution.py:16
  17.0 58.7 %while.32 = (s32[]{:T(128)}, f32[2,9,24,1536]{3,2,1,0:T(8,128)}, f32[2,9,24,1536]{3,2,1,0:T(8,128)}, s32[]{:T(128)}, f32[2,16]{0,1:T(8,128)S(1)}, /*index=5*/bf1...) while((s32[]{:T(128)}, f32[2,9,24,1536]{3,2,1,0:T(8,128)}, ...), condition=%wide.region_2.3_spmd.clone, body=%wide.region_1.2_spmd.clone.sunk | while | flops 4644871 | bytes 17252540 | solution.py:107
  18.7 3.5 %select_add_fusion.6 = (f32[2,9,24,1536]{3,2,1,0:T(8,128)}, f32[2,9,24,1536]{3,2,1,0:T(8,128)}) fusion(f32[2,9,24,1536]{3,2,1,0:T(8,128)} %get-tuple-element.490, f32[9,24,1536]{2,1,0:T(8,128)S(1)} %get-tuple-element.463, f32[2]{0:T(128)S(1)} %fusion.65, pred[]{:T(512)S(6)} %compare.12, f32[9,24,1536]{2,1,0:T(8,128)S(1)} %get-tuple-element.464, ...), kind=kLoop, calls=%fused_computation.clone.1 | loop fusion | flops 3981312 | bytes 13271049 | tf_op jit(solution)/shard_map/while/body/eval_jaxpr/add | solution.py:104
  23.8 6.0 %select_add_fusion.6 = (f32[2,9,24,1536]{3,2,1,0:T(8,128)}, f32[2,9,24,1536]{3,2,1,0:T(8,128)}) fusion(f32[2,9,24,1536]{3,2,1,0:T(8,128)} %get-tuple-element.490, f32[9,24,1536]{2,1,0:T(8,128)S(1)} %get-tuple-element.463, f32[2]{0:T(128)S(1)} %fusion.65, pred[]{:T(512)S(6)} %compare.12, f32[9,24,1536]{2,1,0:T(8,128)S(1)} %get-tuple-element.464, ...), kind=kLoop, calls=%fused_computation.clone.1 | loop fusion | flops 3981312 | bytes 13271049 | tf_op jit(solution)/shard_map/while/body/eval_jaxpr/add | solution.py:104
  31.4 6.0 %select_add_fusion.6 = (f32[2,9,24,1536]{3,2,1,0:T(8,128)}, f32[2,9,24,1536]{3,2,1,0:T(8,128)}) fusion(f32[2,9,24,1536]{3,2,1,0:T(8,128)} %get-tuple-element.490, f32[9,24,1536]{2,1,0:T(8,128)S(1)} %get-tuple-element.463, f32[2]{0:T(128)S(1)} %fusion.65, pred[]{:T(512)S(6)} %compare.12, f32[9,24,1536]{2,1,0:T(8,128)S(1)} %get-tuple-element.464, ...), kind=kLoop, calls=%fused_computation.clone.1 | loop fusion | flops 3981312 | bytes 13271049 | tf_op jit(solution)/shard_map/while/body/eval_jaxpr/add | solution.py:104
  39.1 6.0 %select_add_fusion.6 = (f32[2,9,24,1536]{3,2,1,0:T(8,128)}, f32[2,9,24,1536]{3,2,1,0:T(8,128)}) fusion(f32[2,9,24,1536]{3,2,1,0:T(8,128)} %get-tuple-element.490, f32[9,24,1536]{2,1,0:T(8,128)S(1)} %get-tuple-element.463, f32[2]{0:T(128)S(1)} %fusion.65, pred[]{:T(512)S(6)} %compare.12, f32[9,24,1536]{2,1,0:T(8,128)S(1)} %get-tuple-element.464, ...), kind=kLoop, calls=%fused_computation.clone.1 | loop fusion | flops 3981312 | bytes 13271049 | tf_op jit(solution)/shard_map/while/body/eval_jaxpr/add | solution.py:104
  46.7 6.0 %select_add_fusion.6 = (f32[2,9,24,1536]{3,2,1,0:T(8,128)}, f32[2,9,24,1536]{3,2,1,0:T(8,128)}) fusion(f32[2,9,24,1536]{3,2,1,0:T(8,128)} %get-tuple-element.490, f32[9,24,1536]{2,1,0:T(8,128)S(1)} %get-tuple-element.463, f32[2]{0:T(128)S(1)} %fusion.65, pred[]{:T(512)S(6)} %compare.12, f32[9,24,1536]{2,1,0:T(8,128)S(1)} %get-tuple-element.464, ...), kind=kLoop, calls=%fused_computation.clone.1 | loop fusion | flops 3981312 | bytes 13271049 | tf_op jit(solution)/shard_map/while/body/eval_jaxpr/add | solution.py:104
  54.4 6.0 %select_add_fusion.6 = (f32[2,9,24,1536]{3,2,1,0:T(8,128)}, f32[2,9,24,1536]{3,2,1,0:T(8,128)}) fusion(f32[2,9,24,1536]{3,2,1,0:T(8,128)} %get-tuple-element.490, f32[9,24,1536]{2,1,0:T(8,128)S(1)} %get-tuple-element.463, f32[2]{0:T(128)S(1)} %fusion.65, pred[]{:T(512)S(6)} %compare.12, f32[9,24,1536]{2,1,0:T(8,128)S(1)} %get-tuple-element.464, ...), kind=kLoop, calls=%fused_computation.clone.1 | loop fusion | flops 3981312 | bytes 13271049 | tf_op jit(solution)/shard_map/while/body/eval_jaxpr/add | solution.py:104
  62.0 6.0 %select_add_fusion.6 = (f32[2,9,24,1536]{3,2,1,0:T(8,128)}, f32[2,9,24,1536]{3,2,1,0:T(8,128)}) fusion(f32[2,9,24,1536]{3,2,1,0:T(8,128)} %get-tuple-element.490, f32[9,24,1536]{2,1,0:T(8,128)S(1)} %get-tuple-element.463, f32[2]{0:T(128)S(1)} %fusion.65, pred[]{:T(512)S(6)} %compare.12, f32[9,24,1536]{2,1,0:T(8,128)S(1)} %get-tuple-element.464, ...), kind=kLoop, calls=%fused_computation.clone.1 | loop fusion | flops 3981312 | bytes 13271049 | tf_op jit(solution)/shard_map/while/body/eval_jaxpr/add | solution.py:104
  69.7 6.0 %select_add_fusion.6 = (f32[2,9,24,1536]{3,2,1,0:T(8,128)}, f32[2,9,24,1536]{3,2,1,0:T(8,128)}) fusion(f32[2,9,24,1536]{3,2,1,0:T(8,128)} %get-tuple-element.490, f32[9,24,1536]{2,1,0:T(8,128)S(1)} %get-tuple-element.463, f32[2]{0:T(128)S(1)} %fusion.65, pred[]{:T(512)S(6)} %compare.12, f32[9,24,1536]{2,1,0:T(8,128)S(1)} %get-tuple-element.464, ...), kind=kLoop, calls=%fused_computation.clone.1 | loop fusion | flops 3981312 | bytes 13271049 | tf_op jit(solution)/shard_map/while/body/eval_jaxpr/add | solution.py:104
  75.8 59.5 %while.33 = (s32[]{:T(128)}, f32[2,9,24,1536]{3,2,1,0:T(8,128)}, f32[2,9,24,1536]{3,2,1,0:T(8,128)}, s32[]{:T(128)}, f32[2,16]{0,1:T(8,128)S(1)}, /*index=5*/bf1...) while((s32[]{:T(128)}, f32[2,9,24,1536]{3,2,1,0:T(8,128)}, ...), condition=%wide.region_4.5_spmd.clone, body=%wide.region_3.4_spmd.clone.sunk | while | flops 4644871 | bytes 17252540 | solution.py:107
  77.4 3.6 %select_add_fusion.7 = (f32[2,9,24,1536]{3,2,1,0:T(8,128)}, f32[2,9,24,1536]{3,2,1,0:T(8,128)}) fusion(f32[2,9,24,1536]{3,2,1,0:T(8,128)} %get-tuple-element.520, f32[9,24,1536]{2,1,0:T(8,128)S(1)} %get-tuple-element.474, f32[2]{0:T(128)S(1)} %fusion.66, pred[]{:T(512)S(6)} %compare.13, f32[9,24,1536]{2,1,0:T(8,128)S(1)} %get-tuple-element.475, ...), kind=kLoop, calls=%fused_computation.6.clone.1 | loop fusion | flops 3981312 | bytes 13271049 | tf_op jit(solution)/shard_map/while/body/eval_jaxpr/add | solution.py:104
  82.6 6.1 %select_add_fusion.7 = (f32[2,9,24,1536]{3,2,1,0:T(8,128)}, f32[2,9,24,1536]{3,2,1,0:T(8,128)}) fusion(f32[2,9,24,1536]{3,2,1,0:T(8,128)} %get-tuple-element.520, f32[9,24,1536]{2,1,0:T(8,128)S(1)} %get-tuple-element.474, f32[2]{0:T(128)S(1)} %fusion.66, pred[]{:T(512)S(6)} %compare.13, f32[9,24,1536]{2,1,0:T(8,128)S(1)} %get-tuple-element.475, ...), kind=kLoop, calls=%fused_computation.6.clone.1 | loop fusion | flops 3981312 | bytes 13271049 | tf_op jit(solution)/shard_map/while/body/eval_jaxpr/add | solution.py:104
  90.4 6.1 %select_add_fusion.7 = (f32[2,9,24,1536]{3,2,1,0:T(8,128)}, f32[2,9,24,1536]{3,2,1,0:T(8,128)}) fusion(f32[2,9,24,1536]{3,2,1,0:T(8,128)} %get-tuple-element.520, f32[9,24,1536]{2,1,0:T(8,128)S(1)} %get-tuple-element.474, f32[2]{0:T(128)S(1)} %fusion.66, pred[]{:T(512)S(6)} %compare.13, f32[9,24,1536]{2,1,0:T(8,128)S(1)} %get-tuple-element.475, ...), kind=kLoop, calls=%fused_computation.6.clone.1 | loop fusion | flops 3981312 | bytes 13271049 | tf_op jit(solution)/shard_map/while/body/eval_jaxpr/add | solution.py:104
  98.1 6.1 %select_add_fusion.7 = (f32[2,9,24,1536]{3,2,1,0:T(8,128)}, f32[2,9,24,1536]{3,2,1,0:T(8,128)}) fusion(f32[2,9,24,1536]{3,2,1,0:T(8,128)} %get-tuple-element.520, f32[9,24,1536]{2,1,0:T(8,128)S(1)} %get-tuple-element.474, f32[2]{0:T(128)S(1)} %fusion.66, pred[]{:T(512)S(6)} %compare.13, f32[9,24,1536]{2,1,0:T(8,128)S(1)} %get-tuple-element.475, ...), kind=kLoop, calls=%fused_computation.6.clone.1 | loop fusion | flops 3981312 | bytes 13271049 | tf_op jit(solution)/shard_map/while/body/eval_jaxpr/add | solution.py:104
  105.9 6.1 %select_add_fusion.7 = (f32[2,9,24,1536]{3,2,1,0:T(8,128)}, f32[2,9,24,1536]{3,2,1,0:T(8,128)}) fusion(f32[2,9,24,1536]{3,2,1,0:T(8,128)} %get-tuple-element.520, f32[9,24,1536]{2,1,0:T(8,128)S(1)} %get-tuple-element.474, f32[2]{0:T(128)S(1)} %fusion.66, pred[]{:T(512)S(6)} %compare.13, f32[9,24,1536]{2,1,0:T(8,128)S(1)} %get-tuple-element.475, ...), kind=kLoop, calls=%fused_computation.6.clone.1 | loop fusion | flops 3981312 | bytes 13271049 | tf_op jit(solution)/shard_map/while/body/eval_jaxpr/add | solution.py:104
  113.7 6.1 %select_add_fusion.7 = (f32[2,9,24,1536]{3,2,1,0:T(8,128)}, f32[2,9,24,1536]{3,2,1,0:T(8,128)}) fusion(f32[2,9,24,1536]{3,2,1,0:T(8,128)} %get-tuple-element.520, f32[9,24,1536]{2,1,0:T(8,128)S(1)} %get-tuple-element.474, f32[2]{0:T(128)S(1)} %fusion.66, pred[]{:T(512)S(6)} %compare.13, f32[9,24,1536]{2,1,0:T(8,128)S(1)} %get-tuple-element.475, ...), kind=kLoop, calls=%fused_computation.6.clone.1 | loop fusion | flops 3981312 | bytes 13271049 | tf_op jit(solution)/shard_map/while/body/eval_jaxpr/add | solution.py:104
  121.4 6.1 %select_add_fusion.7 = (f32[2,9,24,1536]{3,2,1,0:T(8,128)}, f32[2,9,24,1536]{3,2,1,0:T(8,128)}) fusion(f32[2,9,24,1536]{3,2,1,0:T(8,128)} %get-tuple-element.520, f32[9,24,1536]{2,1,0:T(8,128)S(1)} %get-tuple-element.474, f32[2]{0:T(128)S(1)} %fusion.66, pred[]{:T(512)S(6)} %compare.13, f32[9,24,1536]{2,1,0:T(8,128)S(1)} %get-tuple-element.475, ...), kind=kLoop, calls=%fused_computation.6.clone.1 | loop fusion | flops 3981312 | bytes 13271049 | tf_op jit(solution)/shard_map/while/body/eval_jaxpr/add | solution.py:104
  129.2 6.1 %select_add_fusion.7 = (f32[2,9,24,1536]{3,2,1,0:T(8,128)}, f32[2,9,24,1536]{3,2,1,0:T(8,128)}) fusion(f32[2,9,24,1536]{3,2,1,0:T(8,128)} %get-tuple-element.520, f32[9,24,1536]{2,1,0:T(8,128)S(1)} %get-tuple-element.474, f32[2]{0:T(128)S(1)} %fusion.66, pred[]{:T(512)S(6)} %compare.13, f32[9,24,1536]{2,1,0:T(8,128)S(1)} %get-tuple-element.475, ...), kind=kLoop, calls=%fused_computation.6.clone.1 | loop fusion | flops 3981312 | bytes 13271049 | tf_op jit(solution)/shard_map/while/body/eval_jaxpr/add | solution.py:104
  137.6 1.8 fusion.11
  144.7 1.9 fusion.20
  146.6 1.9 fusion.23
  148.6 2.1 fusion.26
  150.6 1.9 fusion.29
  152.6 1.9 multiply_convert_fusion
  155.3 2.7 fusion.4
  158.3 58.4 %all_to_all.27 = f32[4,384,2,384]{1,3,2,0:T(8,128)} all-to-all(f32[4,384,2,384]{1,3,2,0:T(8,128)S(1)} %bitcast.119), channel_id=1, replica_groups=mesh['cand'=2,'mp_0'=4,'mp_1'=2,'mp_2'=8,'dp'=2] {'mp_0'}, dimensions={0} | all-to-all | bytes 9437184 | tf_op jit(solution)/shard_map/all_to_all | solution.py:42
  216.7 2.7 reduce_sum.55
  220.9 7.7 %all-to-all-start.2 = ((f32[16,24,2,384]{3,1,2,0:T(8,128)}), f32[16,24,2,384]{3,1,2,0:T(8,128)S(1)}, u32[]{:S(2)}, u32[]{:S(2)}) async-start(f32[16,24,2,384]{3,1,2,0:T(8,128)} %copy.35), calls=%async_computation.2 | async-start | bytes 2359296 | tf_op jit(solution)/shard_map/all_to_all | solution.py:42
  228.7 29.1 %all-to-all-done.2 = f32[16,24,2,384]{3,1,2,0:T(8,128)S(1)} async-done(((f32[16,24,2,384]{3,1,2,0:T(8,128)}), f32[16,24,2,384]{3,1,2,0:T(8,128)S(1)}, u32[]{:S(2)}, u32[]{:S(2)}) %all-to-all-start.2) | async-done | bytes 1179680 | tf_op jit(solution)/shard_map/all_to_all | solution.py:42
  258.5 15.8 %all_to_all.28 = f32[16,1,2]{2,1,0:T(1,128)S(1)} all-to-all(f32[16,1,2]{2,1,0:T(1,128)S(1)} %broadcast_in_dim.109), channel_id=1, replica_groups=mesh['cand'=2,'mp_0'=4,'mp_1'=2,'mp_2'=8,'dp'=2] {'mp_2','dp'}, dimensions={0} | all-to-all | bytes 256 | tf_op jit(solution)/shard_map/all_to_all | solution.py:16
  274.3 8.7 %all_to_all.29 = f32[8,1,2]{2,1,0:T(1,128)S(1)} all-to-all(f32[8,1,2]{2,1,0:T(1,128)S(1)} %broadcast_in_dim.110), channel_id=1, replica_groups=mesh['cand'=2,'mp_0'=4,'mp_1'=2,'mp_2'=8,'dp'=2] {'mp_0','mp_1'}, dimensions={0} | all-to-all | bytes 128 | tf_op jit(solution)/shard_map/all_to_all | solution.py:16
  (95 shorter events, 40.3 us)
Async XLA Ops:
  0.6 15.9 %copy-start.3 = (f32[2,8]{1,0:T(2,128)S(1)}, f32[2,8]{1,0:T(2,128)}, u32[]{:S(2)}) copy-start(f32[2,8]{1,0:T(2,128)} %param.16) | copy-start | bytes 196
  0.6 15.9 %copy-start.4 = (s32[2,8]{1,0:T(2,128)S(1)}, s32[2,8]{1,0:T(2,128)}, u32[]{:S(2)}) copy-start(s32[2,8]{1,0:T(2,128)} %param.17) | copy-start | bytes 196
  3.4 132.4 %all-to-all-start = ((bf16[64,24,384]{2,1,0:T(8,128)(2,1)}), bf16[64,24,384]{2,1,0:T(8,128)(2,1)}, u32[]{:S(2)}, u32[]{:S(2)}) async-start(bf16[64,24,384]{2,1,0:T(8,128)(2,1)} %broadcast_in_dim.92), calls=%async_computation | async-start | bytes 2359296 | tf_op jit(solution)/shard_map/all_to_all | solution.py:16
  16.7 59.0 %collective-permute-start = (f32[2,16]{1,0:T(2,128)S(1)}, f32[2,16]{1,0:T(2,128)S(1)}, u32[]{:S(2)}, u32[]{:S(2)}) collective-permute-start(f32[2,16]{1,0:T(2,128)S(1)} %select_reduce_fusion), channel_id=1, source_target_pairs={{0,128},{128,0},{1,129},{129,1},{2,130},{130,2},{3,131},{131,3},{4... | collective-permute-start | bytes 392 | tf_op jit(solution)/shard_map/ppermute | solution.py:31
  135.3 17.3 %collective-permute-start.1 = (f32[2,9,24,1536]{3,2,1,0:T(8,128)}, f32[2,9,24,1536]{3,2,1,0:T(8,128)S(1)}, u32[]{:S(2)}, u32[]{:S(2)}) collective-permute-start(f32[2,9,24,1536]{3,2,1,0:T(8,128)} %get-tuple-element.253), channel_id=1, source_target_pairs={{0,128},{128,0},{1,129},{129,1},{2,130},{130,2},{3,131},{131,3},{4... | collective-permute-start | bytes 7962632 | tf_op jit(solution)/shard_map/ppermute | solution.py:31
  135.8 19.5 %collective-permute-start.2 = (f32[2,9,24,1536]{3,2,1,0:T(8,128)}, f32[2,9,24,1536]{3,2,1,0:T(8,128)}, u32[]{:S(2)}, u32[]{:S(2)}) collective-permute-start(f32[2,9,24,1536]{3,2,1,0:T(8,128)} %get-tuple-element.255), channel_id=1, source_target_pairs={{0,128},{128,0},{1,129},{129,1},{2,130},{130,2},{3,131},{131,3},{4... | collective-permute-start | bytes 7962632 | tf_op jit(solution)/shard_map/ppermute | solution.py:31
  148.5 4.0 %copy-start = (f32[2,9,24,1536]{3,2,1,0:T(8,128)S(1)}, f32[2,9,24,1536]{3,2,1,0:T(8,128)}, u32[]{:S(2)}) copy-start(f32[2,9,24,1536]{3,2,1,0:T(8,128)} %get-tuple-element.252) | copy-start | bytes 7962628
  152.6 2.7 copy-start.1
  219.8 8.8 %copy-start.2 = (bf16[24,384]{1,0:T(8,128)(2,1)S(1)}, bf16[24,384]{1,0:T(8,128)(2,1)}, u32[]{:S(2)}) copy-start(bf16[24,384]{1,0:T(8,128)(2,1)} %param.11) | copy-start | bytes 55300
  220.9 36.9 %all-to-all-start.2 = ((f32[16,24,2,384]{3,1,2,0:T(8,128)}), f32[16,24,2,384]{3,1,2,0:T(8,128)S(1)}, u32[]{:S(2)}, u32[]{:S(2)}) async-start(f32[16,24,2,384]{3,1,2,0:T(8,128)} %copy.35), calls=%async_computation.2 | async-start | bytes 2359296 | tf_op jit(solution)/shard_map/all_to_all | solution.py:42
where the time goes:
time: 285 us; the launch traced here: 284 us
  other arithmetic  141 us (49%)
  blocking collectives  82.9 us (29%)
  waiting for transfers between devices  29.1 us (10%)
  starting transfers between devices  21.5 us (8%)
  matrix products  4.59 us (2%)
  local copies, waits for them, and re-layouts  3.33 us (1%)
    add x16, other arithmetic, accumulate(): totals[1] + coeff * second_snap[None]  92.1 us
    all_to_all x1, blocking collectives, sum_at_owner(): lax.all_to_all(pieces, axis, split_axis=0, concat_axis=0, tiled=True)  58.4 us
    all_to_all x1, waiting for transfers between devices, sum_at_owner(): lax.all_to_all(pieces, axis, split_axis=0, concat_axis=0, tiled=True)  29.1 us
    mul x16, other arithmetic, accumulate(): coeff * second_snap[None]  25.7 us
    all_to_all x2, blocking collectives, sent_to_all(): return lax.all_to_all(copies, axis, split_axis=0, concat_axis=0, tiled=True)  24.5 us
    unnamed x20, other arithmetic  15.5 us
    all_to_all x1, starting transfers between devices, sent_to_all(): return lax.all_to_all(copies, axis, split_axis=0, concat_axis=0, tiled=True)  13.2 us
    all_to_all x1, starting transfers between devices, sum_at_owner(): lax.all_to_all(pieces, axis, split_axis=0, concat_axis=0, tiled=True)  7.73 us
  transfers between devices with their start and end apart: 5, of which 1 were waited for; matrix products, arithmetic and copies ran while one was open for 49% of the time, Pallas kernels for 0%

commit v1 on v0

--- a/solution.py
+++ b/solution.py
@@ -1,6 +1,8 @@
 import jax
 import jax.numpy as jnp
 from jax import lax
+from jax.experimental import pallas as pl
+from jax.experimental.pallas import tpu as pltpu
 from jax.sharding import Mesh
 from jax.sharding import PartitionSpec as P
 
@@ -87,24 +89,110 @@
     )
 
 
-def blend_owned(first_own, second_own, mixing, first_slot):
-    members = mixing.shape[0]
-    shape = (members,) + first_own.shape[1:]
-
-    def accumulate(which, totals):
-        coeff = lax.dynamic_slice_in_dim(mixing, first_slot + which, 1, 1)[:, 0][
-            :, None, None, None
-        ]
-        first_snap = lax.dynamic_index_in_dim(first_own, which, 0, keepdims=False).astype(
-            jnp.float32
-        )
-        second_snap = lax.dynamic_index_in_dim(second_own, which, 0, keepdims=False).astype(
-            jnp.float32
-        )
-        return (totals[0] + coeff * first_snap[None], totals[1] + coeff * second_snap[None])
-
-    empty = jnp.zeros(shape, jnp.float32)
-    return lax.fori_loop(0, first_own.shape[0], accumulate, (empty, empty))
+MIB = 1024 * 1024
+
+
+def blend_kernel(mix_ref, snap_ref, mine_ref, give_ref):
+    snaps, _, _, width = snap_ref.shape
+    members = mine_ref.shape[0]
+    step = 256
+
+    @pl.loop(0, width // step)
+    def _(j):
+        cols = pl.ds(pl.multiple_of(j * step, step), step)
+        totals = [None] * (2 * members)
+        for k in range(snaps):
+            values = snap_ref[k, 0, :, cols].astype(jnp.float32)
+            for row in range(2 * members):
+                term = mix_ref[row, k] * values
+                totals[row] = term if totals[row] is None else totals[row] + term
+        for row in range(members):
+            mine_ref[row, 0, :, cols] = totals[row]
+            give_ref[row, 0, :, cols] = totals[members + row]
+
+
+def blend_owned(snap_own, mix_rows):
+    snaps, taps, rows, width = snap_own.shape
+    members = mix_rows.shape[0] // 2
+    out = jax.ShapeDtypeStruct((members, taps, rows, width), jnp.float32)
+    spec = pl.BlockSpec((members, 1, rows, width), lambda k: (0, k, 0, 0))
+    return pl.pallas_call(
+        blend_kernel,
+        grid=(taps,),
+        out_shape=(out, out),
+        in_specs=[
+            pl.BlockSpec(memory_space=pltpu.SMEM),
+            pl.BlockSpec((snaps, 1, rows, width), lambda k: (0, k, 0, 0)),
+        ],
+        out_specs=(spec, spec),
+        cost_estimate=pl.CostEstimate(
+            flops=16 * taps * rows * width * snaps,
+            bytes_accessed=2 * snaps * taps * rows * width + 16 * members * taps * rows * width // 2,
+            transcendentals=0,
+        ),
+        name="blend",
+    )(mix_rows, snap_own)
+
+
+def shifted(values, down_by, right_by):
+    tokens = values.shape[1]
+    offset = down_by * 8 + right_by
+    moved = values if offset == 0 else pltpu.roll(values, (-offset) % tokens, 1)
+    token = lax.broadcasted_iota(jnp.int32, values.shape, 1)
+    row = ((token >> 3) & 7) + down_by
+    col = (token & 7) + right_by
+    inside = (row >= 0) & (row < 8) & (col >= 0) & (col < 8)
+    return jnp.where(inside, moved, 0.0)
+
+
+TAPS = [(a, b) for a in (-1, 0, 1) for b in (-1, 0, 1)]
+
+
+def first_kernel(w_ref, x_ref, hidden_ref, acc_ref):
+    step = pl.program_id(0)
+    part = jnp.dot(w_ref[...], x_ref[...], preferred_element_type=jnp.float32)
+
+    @pl.when(step == 0)
+    def _():
+        acc_ref[...] = part
+
+    @pl.when(step > 0)
+    def _():
+        acc_ref[...] += part
+
+    @pl.when(step == pl.num_programs(0) - 1)
+    def _():
+        members, rows, _ = hidden_ref.shape
+        for c in range(members):
+            total = None
+            for k, (a, b) in enumerate(TAPS):
+                start = (c * len(TAPS) + k) * rows
+                term = shifted(acc_ref[start : start + rows, :], a, b)
+                total = term if total is None else total + term
+            hidden_ref[c] = (total * (1.0 / (1.0 + jnp.exp(-total)))).astype(jnp.bfloat16)
+
+
+def first_layer(w, x):
+    members, taps, rows, width = w.shape
+    tokens = x.shape[1]
+    step = 256
+    return pl.pallas_call(
+        first_kernel,
+        grid=(width // step,),
+        out_shape=jax.ShapeDtypeStruct((members, rows, tokens), jnp.bfloat16),
+        in_specs=[
+            pl.BlockSpec((members * taps * rows, step), lambda i: (0, i)),
+            pl.BlockSpec((step, tokens), lambda i: (i, 0)),
+        ],
+        out_specs=pl.BlockSpec((members, rows, tokens), lambda i: (0, 0, 0)),
+        scratch_shapes=[pltpu.VMEM((members * taps * rows, tokens), jnp.float32)],
+        cost_estimate=pl.CostEstimate(
+            flops=2 * members * taps * rows * width * tokens,
+            bytes_accessed=2 * members * taps * rows * width + 2 * width * tokens,
+            transcendentals=members * rows * tokens,
+        ),
+        name="first_layer",
+    )(w.reshape(members * taps * rows, width), x)
 
 
 def on_device(clean, noise, level_index, snap_first, snap_second, blend, snap_index):
@@ -118,7 +206,6 @@
     noisy = clean_f + sigmas * noise.astype(jnp.float32)
     x_own = (scale_in * noisy).astype(jnp.bfloat16)
     x_full = gathered_copies(x_own, MP, 0)
-    x_stack = tap_stack(x_full)
     owned = snap_first.shape[0]
     stored = owned * lax.axis_size("cand")
     onehot = (snap_index[:, :, None] == jnp.arange(stored, dtype=jnp.int32)[None, None, :]).astype(
@@ -127,13 +214,16 @@
     mixing = jnp.sum(blend[:, :, None] * onehot, 1)
     first_slot = lax.axis_index("cand") * owned
     other_mix = from_partner(mixing, "cand", 0)
-    mine_first, mine_second = blend_owned(snap_first, snap_second, mixing, first_slot)
-    give_first, give_second = blend_owned(snap_first, snap_second, other_mix, first_slot)
-    got_first, got_second = from_partner((give_first, give_second), "cand", 0)
+    mix_rows = lax.dynamic_slice_in_dim(
+        jnp.concatenate([mixing, other_mix], 0), first_slot, owned, 1
+    )
+    mine_first, give_first = blend_owned(snap_first, mix_rows)
+    got_first = from_partner(give_first, "cand", 0)
+    mine_second, give_second = blend_owned(snap_second, mix_rows)
+    got_second = from_partner(give_second, "cand", 0)
     first_w = (mine_first + got_first).astype(jnp.bfloat16)
     second_w = (mine_second + got_second).astype(jnp.bfloat16)
-    preact = jnp.einsum("gkoc,kct->got", first_w, x_stack, preferred_element_type=jnp.float32)
-    hidden = jax.nn.silu(preact).astype(jnp.bfloat16)
+    hidden = first_layer(first_w, x_full)
     h_stack = tap_stack(hidden)
     shares = summed_rows(
         jnp.einsum("gkio,kgit->ogt", second_w, h_stack, preferred_element_type=jnp.float32),
@@ -146,7 +236,7 @@
         weighting[None, None, :] * (denoised_f - clean_f[None]) ** 2, axis=(1, 2)
     )
     entries = clean.shape[0] * lax.axis_size(MP) * clean.shape[1] * lax.axis_size("dp")
-    totals = over_axes(partial_value, (("mp_0", "mp_1"), ("mp_2", "dp")))
+    totals = over_copies(partial_value, (*MP, "dp"))
     losses = totals / entries
     return (losses, denoised_f.astype(jnp.bfloat16))
 

time: 285 us -> 193 us (0.68)
  other arithmetic: 141 us -> 16.7 us
  Pallas kernels: 0 us -> 24.1 us
  waiting for transfers between devices: 29.1 us -> 47.2 us
  blocking collectives: 82.9 us -> 75.7 us
    add x16 -> x0, other arithmetic: 92.1 us -> none  [accumulate(): totals[1] + coeff * second_snap[None]]
    mul x16 -> x0, other arithmetic: 25.7 us -> none  [accumulate(): coeff * second_snap[None]]
    pallas_call x0 -> x3, Pallas kernels: none -> 24.1 us  [the longest x2 18.6 us: blend_owned(): pl.pallas_call(blend_kernel, grid=(taps,), out_shape=(out, out), in_specs...]
    all_to_all x1, waiting for transfers between devices: 0.01 us -> 17.6 us  [sent_to_all(): return lax.all_to_all(copies, axis, split_axis=0, concat_axis=0, tiled=True)]
    unnamed x20 -> x8, other arithmetic: 15.5 us -> 6.78 us
    all_to_all x2 -> x1, blocking collectives: 24.5 us -> 19.6 us  [sent_to_all(): return lax.all_to_all(copies, axis, split_axis=0, concat_axis=0, tiled=True)]
    convert_element_type x0 -> x1, other arithmetic: none -> 3.97 us  [on_device(): first_w = (mine_first + got_first).astype(jnp.bfloat16)]
  transfers between devices with their start and end apart: 5 -> 5, of which waited for: 1 -> 3; matrix products, arithmetic and copies ran while one was open for 49% -> 7% of each run, Pallas kernels for 0% -> 8%
where the time goes in v1:
time: 193 us; the launch traced here: 192 us
  blocking collectives  75.7 us (39%)
  waiting for transfers between devices  47.2 us (24%)
  Pallas kernels  24.1 us (12%)
  starting transfers between devices  19.3 us (10%)
  other arithmetic  16.7 us (9%)
  local copies, waits for them, and re-layouts  4.84 us (3%)
  matrix products  3.4 us (2%)
    all_to_all x1, blocking collectives, sum_at_owner(): lax.all_to_all(pieces, axis, split_axis=0, concat_axis=0, tiled=True)  56.1 us
    all_to_all x1, waiting for transfers between devices, sum_at_owner(): lax.all_to_all(pieces, axis, split_axis=0, concat_axis=0, tiled=True)  28.4 us
    all_to_all x1, blocking collectives, sent_to_all(): return lax.all_to_all(copies, axis, split_axis=0, concat_axis=0, tiled=True)  19.6 us
    pallas_call x2, Pallas kernels, blend_owned(): pl.pallas_call(blend_kernel, grid=(taps,), out_shape=(out, out), in_specs...  18.6 us
    all_to_all x1, waiting for transfers between devices, sent_to_all(): return lax.all_to_all(copies, axis, split_axis=0, concat_axis=0, tiled=True)  17.6 us
    all_to_all x1, starting transfers between devices, sent_to_all(): return lax.all_to_all(copies, axis, split_axis=0, concat_axis=0, tiled=True)  13 us
    unnamed x8, other arithmetic  6.78 us
    all_to_all x1, starting transfers between devices, sum_at_owner(): lax.all_to_all(pieces, axis, split_axis=0, concat_axis=0, tiled=True)  5.97 us
  transfers between devices with their start and end apart: 5, of which 3 were waited for; matrix products, arithmetic and copies ran while one was open for 7% of the time, Pallas kernels for 8%

profile of v1, /device:TPU:8, one launch (start us, length us, event | category | flops | bytes accessed | tf_op | source)
XLA Modules:
  0.0 191.9 jit_solution(18321799823188624921)
XLA Ops:
  0.6 0.8 select_reduce_fusion
  1.5 1.1 collective-permute-done
  2.7 0.7 constant_dynamic-slice_fusion.mix_ref
  3.3 9.3 %blend.2 = (f32[2,9,24,1536]{3,2,1,0:T(8,128)}, f32[2,9,24,1536]{3,2,1,0:T(8,128)}) custom-call(f32[4,8]{1,0:T(4,128)} %constant_dynamic-slice_fusion.mix_ref, bf16[8,9,24,1536]{3,2,1,0:T(8,128)(2,1)} %snap_ref.2), custom_call_target="tpu_custom_call" | custom-call | flops 42467328 | bytes 10616832 | tf_op jit(solution)/shard_map/blend/pallas_call | solution.py:119
  12.6 0.2 collective-permute-start.1
  13.0 1.1 broadcast_in_dim.48
  14.1 13.0 %all-to-all-start = ((bf16[64,24,384]{2,1,0:T(8,128)(2,1)}), bf16[64,24,384]{2,1,0:T(8,128)(2,1)S(1)}, u32[]{:S(2)}, u32[]{:S(2)}) async-start(bf16[64,24,384]{2,1,0:T(8,128)(2,1)} %broadcast_in_dim.48), calls=%async_computation | async-start | bytes 2359296 | tf_op jit(solution)/shard_map/all_to_all | solution.py:18
  27.4 9.3 %blend.3 = (f32[2,9,24,1536]{3,2,1,0:T(8,128)}, f32[2,9,24,1536]{3,2,1,0:T(8,128)}) custom-call(f32[4,8]{1,0:T(4,128)} %constant_dynamic-slice_fusion.mix_ref, bf16[8,9,24,1536]{3,2,1,0:T(8,128)(2,1)} %snap_ref.3), custom_call_target="tpu_custom_call" | custom-call | flops 42467328 | bytes 10616832 | tf_op jit(solution)/shard_map/blend/pallas_call | solution.py:119
  36.7 4.0 %add_convert_fusion.1 = bf16[2,9,24,1536]{3,2,1,0:T(8,128)(2,1)} fusion(f32[2,9,24,1536]{3,2,1,0:T(8,128)} %get-tuple-element.6, f32[2,9,24,1536]{3,2,1,0:T(8,128)} %collective-permute-done.1), kind=kLoop, calls=%fused_computation.2 | loop fusion | flops 1327104 | bytes 6635520 | tf_op jit(solution)/shard_map/convert_element_type | solution.py:224
  40.6 17.6 %all-to-all-done = bf16[64,24,384]{2,1,0:T(8,128)(2,1)S(1)} async-done(((bf16[64,24,384]{2,1,0:T(8,128)(2,1)}), bf16[64,24,384]{2,1,0:T(8,128)(2,1)S(1)}, u32[]{:S(2)}, u32[]{:S(2)}) %all-to-all-start) | async-done | bytes 1179680 | tf_op jit(solution)/shard_map/all_to_all | solution.py:18
  58.3 1.1 copy-done
  59.4 5.4 %first_layer.1 = bf16[2,24,384]{2,1,0:T(8,128)(2,1)} custom-call(bf16[432,1536]{1,0:T(8,128)(2,1)} %bitcast.48, bf16[1536,384]{1,0:T(8,128)(2,1)} %bitcast.49), custom_call_target="tpu_custom_call" | custom-call | flops 509607936 | bytes 2506752 | tf_op jit(solution)/shard_map/first_layer/pallas_call | solution.py:179
  64.8 0.8 fusion.5
  65.7 0.9 fusion.8
  66.5 0.9 fusion.11
  67.4 0.9 fusion.14
  68.3 0.8 bitcast_dynamic-update-slice_fusion
  69.0 0.9 fusion.17
  69.9 0.9 fusion.20
  70.8 0.9 fusion.23
  71.6 0.9 fusion.26
  72.5 3.4 %fusion = f32[2,384,1536,1]{2,1,0,3:T(8,128)S(1)} fusion(bf16[9,2,24,384]{3,2,1,0:T(8,128)(2,1)S(1)} %fusion.26, f32[2,9,24,1536]{3,2,1,0:T(8,128)} %get-tuple-element.8, f32[2,9,24,1536]{3,2,1,0:T(8,128)} %collective-permute-done.2), kind=kOutput, calls=%fused_computation.3 | convolution fusion | flops 510935040 | bytes 10358784 | tf_op jit(solution)/shard_map/gkio,kgit->ogt/dot_general | solution.py:229
  75.9 0.3 copy.39
  76.2 56.1 %all_to_all.21 = f32[4,384,2,384]{1,3,2,0:T(8,128)} all-to-all(f32[4,384,2,384]{1,3,2,0:T(8,128)S(1)} %bitcast.47), channel_id=1, replica_groups=mesh['cand'=2,'mp_0'=4,'mp_1'=2,'mp_2'=8,'dp'=2] {'mp_0'}, dimensions={0} | all-to-all | bytes 9437184 | tf_op jit(solution)/shard_map/all_to_all | solution.py:44
  132.3 2.7 %reduce_sum.46 = f32[384,2,384]{0,2,1:T(8,128)S(1)} reduce(f32[4,384,2,384]{1,3,2,0:T(8,128)} %all_to_all.21, f32[]{:T(128)} %constant.136.clone.1), dimensions={0}, to_apply=%region_1.2 | reduce | flops 884736 | bytes 5898244 | tf_op jit(solution)/shard_map/reduce_sum | solution.py:45
  135.0 0.4 copy.30
  135.4 1.1 copy.31
  136.5 6.0 %all-to-all-start.2 = ((f32[16,24,2,384]{3,1,2,0:T(8,128)}), f32[16,24,2,384]{3,1,2,0:T(8,128)S(1)}, u32[]{:S(2)}, u32[]{:S(2)}) async-start(f32[16,24,2,384]{3,1,2,0:T(8,128)} %copy.31), calls=%async_computation.2 | async-start | bytes 2359296 | tf_op jit(solution)/shard_map/all_to_all | solution.py:44
  142.5 28.4 %all-to-all-done.2 = f32[16,24,2,384]{3,1,2,0:T(8,128)S(1)} async-done(((f32[16,24,2,384]{3,1,2,0:T(8,128)}), f32[16,24,2,384]{3,1,2,0:T(8,128)S(1)}, u32[]{:S(2)}, u32[]{:S(2)}) %all-to-all-start.2) | async-done | bytes 1179680 | tf_op jit(solution)/shard_map/all_to_all | solution.py:44
  171.0 0.6 fusion.27
  171.7 19.6 %all_to_all.22 = f32[128,1,2]{2,1,0:T(1,128)S(1)} all-to-all(f32[128,1,2]{2,1,0:T(1,128)S(1)} %broadcast_in_dim.57), channel_id=1, replica_groups=mesh['cand'=2,'mp_0'=4,'mp_1'=2,'mp_2'=8,'dp'=2] {'mp_0','mp_1','mp_2','..., dimensions={0} | all-to-all | bytes 2048 | tf_op jit(solution)/shard_map/all_to_all | solution.py:18
  191.4 0.5 broadcast_multiply_fusion
  (30 shorter events, 0.7 us)
Async XLA Ops:
  1.4 1.2 collective-permute-start
  3.3 9.5 %copy-start.3 = (s32[6]{0:T(128)S(1)}, s32[6]{0:T(128)}, u32[]{:S(2)}) copy-start(s32[6]{0:T(128)} %param.9) | copy-start | bytes 76
  3.3 9.7 %copy-start.1 = (bf16[24,384]{1,0:T(8,128)(2,1)S(1)}, bf16[24,384]{1,0:T(8,128)(2,1)}, u32[]{:S(2)}) copy-start(bf16[24,384]{1,0:T(8,128)(2,1)} %param.7) | copy-start | bytes 55300
  3.3 9.7 %copy-start.2 = (bf16[24,384]{1,0:T(8,128)(2,1)S(1)}, bf16[24,384]{1,0:T(8,128)(2,1)}, u32[]{:S(2)}) copy-start(bf16[24,384]{1,0:T(8,128)(2,1)} %param.8) | copy-start | bytes 55300
  12.6 24.0 %collective-permute-start.1 = (f32[2,9,24,1536]{3,2,1,0:T(8,128)}, f32[2,9,24,1536]{3,2,1,0:T(8,128)}, u32[]{:S(2)}, u32[]{:S(2)}) collective-permute-start(f32[2,9,24,1536]{3,2,1,0:T(8,128)} %get-tuple-element.7), channel_id=1, source_target_pairs={{0,128},{128,0},{1,129},{129,1},{2,130},{130,2},{3,131},{131,3},{4... | collective-permute-start | bytes 7962632 | tf_op jit(solution)/shard_map/ppermute | solution.py:33
  14.1 44.1 %all-to-all-start = ((bf16[64,24,384]{2,1,0:T(8,128)(2,1)}), bf16[64,24,384]{2,1,0:T(8,128)(2,1)S(1)}, u32[]{:S(2)}, u32[]{:S(2)}) async-start(bf16[64,24,384]{2,1,0:T(8,128)(2,1)} %broadcast_in_dim.48), calls=%async_computation | async-start | bytes 2359296 | tf_op jit(solution)/shard_map/all_to_all | solution.py:18
  36.7 35.8 %collective-permute-start.2 = (f32[2,9,24,1536]{3,2,1,0:T(8,128)}, f32[2,9,24,1536]{3,2,1,0:T(8,128)}, u32[]{:S(2)}, u32[]{:S(2)}) collective-permute-start(f32[2,9,24,1536]{3,2,1,0:T(8,128)} %get-tuple-element.9), channel_id=1, source_target_pairs={{0,128},{128,0},{1,129},{129,1},{2,130},{130,2},{3,131},{131,3},{4... | collective-permute-start | bytes 7962632 | tf_op jit(solution)/shard_map/ppermute | solution.py:33
  58.3 1.1 copy-start
  136.5 34.4 %all-to-all-start.2 = ((f32[16,24,2,384]{3,1,2,0:T(8,128)}), f32[16,24,2,384]{3,1,2,0:T(8,128)S(1)}, u32[]{:S(2)}, u32[]{:S(2)}) async-start(f32[16,24,2,384]{3,1,2,0:T(8,128)} %copy.31), calls=%async_computation.2 | async-start | bytes 2359296 | tf_op jit(solution)/shard_map/all_to_all | solution.py:44

commit v2 on v0

v2 whole, which is shorter than its diff:
```python
import jax
import jax.numpy as jnp
from jax import lax
from jax.experimental import pallas as pl
from jax.experimental.pallas import tpu as pltpu
from jax.sharding import Mesh
from jax.sharding import PartitionSpec as P

LEVELS = 32
MP = ("mp_0", "mp_1", "mp_2")
ROWS = ("mp_0", "mp_1")


SIGMA_DATA = 0.5


def sent_to_all(value, axis):
    copies = jnp.broadcast_to(value, (lax.axis_size(axis), *value.shape))
    return lax.all_to_all(copies, axis, split_axis=0, concat_axis=0, tiled=True)


def from_partner(value, axis, apart):
    return lax.ppermute(value, axis, [(i, i ^ 1 << apart) for i in range(lax.axis_size(axis))])


def over_copies(value, axis):
    return sent_to_all(value, axis).sum(axis=0)


def noise_scale(level_index):
    ratio = 2.0 * level_index.astype(jnp.float32) / (LEVELS - 1) - 1.0
    return jnp.exp(-0.4 + 2.0 * ratio)


def weighted_rows(mix_ref, row, values):
    total = None
    for n, value in enumerate(values):
        term = mix_ref[row, n] * value
        total = term if total is None else total + term
    return total


def give_kernel(mix_ref, start_ref, snap_ref, out_ref, own, totals, in_sems, out_sems):
    snaps, chunks, rows, width = own.shape
    step = 256
    start = start_ref[0]

    def arriving(k):
        span = pl.ds(pl.multiple_of(start + k * rows, 8), rows)
        return pltpu.make_async_copy(snap_ref.at[:, span, :], own.at[:, k], in_sems.at[k])

    def leaving(k):
        span = pl.ds(pl.multiple_of(k * rows, 8), rows)
        return pltpu.make_async_copy(totals.at[:, k], out_ref.at[:, span, :], out_sems.at[k])

    for k in range(chunks):
        arriving(k).start()

    @pl.loop(0, chunks)
    def _(k):
        arriving(k).wait()

        @pl.loop(0, width // step)
        def _(j):
            cols = pl.ds(pl.multiple_of(j * step, step), step)
            values = [own[n, k, :, cols].astype(jnp.float32) for n in range(snaps)]
            for row in range(totals.shape[0]):
                totals[row, k, :, cols] = weighted_rows(mix_ref, row, values)

        leaving(k).start()

    @pl.loop(0, chunks)
    def _(k):
        leaving(k).wait()


ANY = pl.BlockSpec(memory_space=pl.ANY)
SCALARS = pl.BlockSpec(memory_space=pltpu.SMEM)


def given_away(mix, snap, start, chunks, rows):
    snaps, _, width = snap.shape
    members = mix.shape[0]
    return pl.pallas_call(
        give_kernel,
        out_shape=jax.ShapeDtypeStruct((members, chunks * rows, width), jnp.float32),
        in_specs=[SCALARS, SCALARS, ANY],
        out_specs=ANY,
        scratch_shapes=[
            pltpu.VMEM((snaps, chunks, rows, width), jnp.bfloat16),
            pltpu.VMEM((members, chunks, rows, width), jnp.float32),
            pltpu.SemaphoreType.DMA((chunks,)),
            pltpu.SemaphoreType.DMA((chunks,)),
        ],
        cost_estimate=pl.CostEstimate(
            flops=2 * members * chunks * rows * width * snaps,
            bytes_accessed=(2 * snaps + 4 * members) * chunks * rows * width,
            transcendentals=0,
        ),
        name="give",
    )(mix, start.reshape(1), snap)


def keep_kernel(mix_ref, snap_ref, got_ref, out_ref, own, got, kept, in_sems, got_sems, out_sems):
    snaps, chunks, rows, width = own.shape
    step = 256

    def span(k):
        return pl.ds(pl.multiple_of(k * rows, 8), rows)

    def arriving(k):
        return pltpu.make_async_copy(snap_ref.at[:, span(k), :], own.at[:, k], in_sems.at[k])

    def partner(k):
        return pltpu.make_async_copy(got_ref.at[:, span(k), :], got.at[:, k], got_sems.at[k])

    def leaving(k):
        return pltpu.make_async_copy(kept.at[:, k], out_ref.at[:, span(k), :], out_sems.at[k])

    for k in range(chunks):
        arriving(k).start()
        partner(k).start()

    @pl.loop(0, chunks)
    def _(k):
        arriving(k).wait()
        partner(k).wait()

        @pl.loop(0, width // step)
        def _(j):
            cols = pl.ds(pl.multiple_of(j * step, step), step)
            values = [own[n, k, :, cols].astype(jnp.float32) for n in range(snaps)]
            for row in range(kept.shape[0]):
                total = weighted_rows(mix_ref, row, values) + got[row, k, :, cols]
                kept[row, k, :, cols] = total.astype(jnp.bfloat16)

        leaving(k).start()

    @pl.loop(0, chunks)
    def _(k):
        leaving(k).wait()


def kept_first(mix, snap, got, chunks):
    snaps, tall, width = snap.shape
    members = mix.shape[0]
    rows = tall // chunks
    return pl.pallas_call(
        keep_kernel,
        out_shape=jax.ShapeDtypeStruct((members, tall, width), jnp.bfloat16),
        in_specs=[SCALARS, ANY, ANY],
        out_specs=ANY,
        scratch_shapes=[
            pltpu.VMEM((snaps, chunks, rows, width), jnp.bfloat16),
            pltpu.VMEM((members, chunks, rows, width), jnp.float32),
            pltpu.VMEM((members, chunks, rows, width), jnp.bfloat16),
            pltpu.SemaphoreType.DMA((chunks,)),
            pltpu.SemaphoreType.DMA((chunks,)),
            pltpu.SemaphoreType.DMA((chunks,)),
        ],
        cost_estimate=pl.CostEstimate(
            flops=2 * members * tall * width * snaps,
            bytes_accessed=(2 * snaps + 6 * members) * tall * width,
            transcendentals=0,
        ),
        name="keep",
    )(mix, snap, got)


def turn_kernel(mix_ref, start_ref, snap_ref, got_ref, out_ref, own, got, turned, in_sems, got_sems, out_sems):
    pieces, snaps, rows, step = own.shape
    members = got.shape[1]
    owners = out_ref.shape[0]
    each = turned.shape[2]
    start = pl.multiple_of(start_ref[0], 8)

    def cols(k):
        return pl.ds(pl.multiple_of(k * step, step), step)

    def arriving(k):
        source = snap_ref.at[:, pl.ds(start, rows), cols(k)]
        return pltpu.make_async_copy(source, own.at[k], in_sems.at[k])

    def partner(k):
        return pltpu.make_async_copy(got_ref.at[:, :, cols(k)], got.at[k], got_sems.at[k])

    def leaving(g):
        target = out_ref.at[g, :, pl.ds(0, each), :]
        return pltpu.make_async_copy(turned.at[g], target, out_sems.at[g])

    for k in range(pieces):
        arriving(k).start()
        partner(k).start()

    @pl.loop(0, pieces)
    def _(k):
        arriving(k).wait()
        partner(k).wait()
        for part in range(step // 128):
            lanes = slice(part * 128, (part + 1) * 128)
            values = [own[k, n, :, lanes].astype(jnp.float32) for n in range(snaps)]
            for row in range(members):
                total = weighted_rows(mix_ref, row, values) + got[k, row, :, lanes]
                turn = total.T.astype(jnp.bfloat16)
                low = part * 128
                for owner in range(2):
                    first, last = max(low, owner * each), min(low + 128, (owner + 1) * each)
                    if first < last:
                        turned[2 * k + owner, row, first - owner * each : last - owner * each, :] = (
                            turn[first - low : last - low]
                        )
        leaving(2 * k).start()
        leaving(2 * k + 1).start()

    @pl.loop(0, owners)
    def _(g):
        leaving(g).wait()


def turned_second(mix, snap, got, start, extra):
    snaps, _, width = snap.shape
    members, rows, _ = got.shape
    pieces, owners, each = 4, 8, width // 8
    return pl.pallas_call(
        turn_kernel,
        out_shape=jax.ShapeDtypeStruct((owners, members, each + extra, rows), jnp.bfloat16),
        in_specs=[SCALARS, SCALARS, ANY, ANY],
        out_specs=ANY,
        scratch_shapes=[
            pltpu.VMEM((pieces, snaps, rows, width // pieces), jnp.bfloat16),
            pltpu.VMEM((pieces, members, rows, width // pieces), jnp.float32),
            pltpu.VMEM((owners, members, each, rows), jnp.bfloat16),
            pltpu.SemaphoreType.DMA((pieces,)),
            pltpu.SemaphoreType.DMA((pieces,)),
            pltpu.SemaphoreType.DMA((owners,)),
        ],
        cost_estimate=pl.CostEstimate(
            flops=2 * members * rows * width * snaps,
            bytes_accessed=(2 * snaps + 6 * members) * rows * width,
            transcendentals=0,
        ),
        name="turn",
    )(mix, start.reshape(1), snap, got)


TAPS = [(a, b) for a in (-1, 0, 1) for b in (-1, 0, 1)]


def shifted(values, down_by, right_by):
    tokens = values.shape[1]
    offset = down_by * 8 + right_by
    moved = values if offset == 0 else pltpu.roll(values, (-offset) % tokens, 1)
    token = lax.broadcasted_iota(jnp.int32, values.shape, 1)
    row = ((token >> 3) & 7) + down_by
    col = (token & 7) + right_by
    inside = (row >= 0) & (row < 8) & (col >= 0) & (col < 8)
    return jnp.where(inside, moved, 0.0)


def first_kernel(w_ref, x_ref, filled_ref, out_ref, acc_ref, hidden_ref, sems):
    acc_ref[...] = jnp.dot(w_ref[...], x_ref[...], preferred_element_type=jnp.float32)
    owners, members = out_ref.shape[:2]
    rows = acc_ref.shape[0] // (members * len(TAPS))
    lanes = hidden_ref.shape[2]
    tall = hidden_ref.shape[1]

    def leaving(g):
        target = out_ref.at[g, :, pl.ds(out_ref.shape[2] - tall, tall), :]
        return pltpu.make_async_copy(hidden_ref, target, sems.at[g])

    for c in range(members):
        total = None
        for k, (a, b) in enumerate(TAPS):
            start = (c * len(TAPS) + k) * rows
            term = shifted(acc_ref[start : start + rows, :], a, b)
            total = term if total is None else total + term
        total = total * (1.0 / (1.0 + jnp.exp(-total)))
        parts = [total[:, j * lanes : (j + 1) * lanes] for j in range(total.shape[1] // lanes)]
        hidden_ref[c] = jnp.concatenate(parts, 0).astype(jnp.bfloat16)
    for g in range(owners):
        leaving(g).start()
    for g in range(owners):
        leaving(g).wait()


def first_layer(w, x, filled):
    tall, width = w.shape
    tokens = x.shape[1]
    owners, members, _, lanes = filled.shape
    rows = tall // (members * len(TAPS))
    extra = rows * tokens // lanes
    whole = pl.BlockSpec(memory_space=pltpu.VMEM)
    return pl.pallas_call(
        first_kernel,
        out_shape=jax.ShapeDtypeStruct(filled.shape, filled.dtype),
        in_specs=[whole, whole, ANY],
        out_specs=ANY,
        input_output_aliases={2: 0},
        scratch_shapes=[
            pltpu.VMEM((tall, tokens), jnp.float32),
            pltpu.VMEM((members, extra, lanes), jnp.bfloat16),
            pltpu.SemaphoreType.DMA((owners,)),
        ],
        cost_estimate=pl.CostEstimate(
            flops=2 * tall * width * tokens,
            bytes_accessed=2 * tall * width + 2 * width * tokens,
            transcendentals=members * rows * tokens,
        ),
        name="first_layer",
    )(w, x, filled)


def second_kernel(got_ref, out_ref, acc_ref):
    sources, halves, _, lanes = got_ref.shape
    owners, _, rows, tokens = out_ref.shape
    each = owners * rows
    cut = lanes
    blank = jnp.zeros((halves * lanes - len(TAPS) * rows, tokens), jnp.float32)
    for half in range(halves):
        total = None
        for s in range(sources):
            parts = [
                got_ref[s, half, each + j * rows : each + (j + 1) * rows, :].astype(jnp.float32)
                for j in range(tokens // lanes)
            ]
            h = jnp.concatenate(parts, 1)
            stack = jnp.concatenate([shifted(h, a, b) for a, b in TAPS], 0)
            stack = jnp.concatenate([stack[:cut], blank, stack[cut:]], 0).astype(jnp.bfloat16)
            w = jnp.concatenate([got_ref[s, 0, :each, :], got_ref[s, 1, :each, :]], 1)
            term = jnp.dot(w, stack, preferred_element_type=jnp.float32)
            total = term if total is None else total + term
        acc_ref[...] = total
        for z in range(owners):
            out_ref[z, half] = acc_ref[z * rows : (z + 1) * rows, :]


def second_layer(got, rows, tokens):
    sources, halves, _, lanes = got.shape
    whole = pl.BlockSpec(memory_space=pltpu.VMEM)
    return pl.pallas_call(
        second_kernel,
        out_shape=jax.ShapeDtypeStruct((8, halves, rows, tokens), jnp.float32),
        in_specs=[whole],
        out_specs=whole,
        scratch_shapes=[pltpu.VMEM((8 * rows, tokens), jnp.float32)],
        cost_estimate=pl.CostEstimate(
            flops=2 * sources * 8 * rows * 256 * 2 * tokens,
            bytes_accessed=2 * got.size + 4 * 16 * rows * tokens,
            transcendentals=0,
        ),
        name="second_layer",
    )(got)


def on_device(clean, noise, level_index, snap_first, snap_second, blend, snap_index):
    side = lax.axis_index("dp").astype(jnp.int32)
    sigmas = jnp.repeat(noise_scale(level_index), 64)
    spread = sigmas * sigmas + SIGMA_DATA * SIGMA_DATA
    scale_in = 1.0 / jnp.sqrt(spread)
    scale_skip = SIGMA_DATA * SIGMA_DATA / spread
    scale_out = sigmas * SIGMA_DATA / jnp.sqrt(spread)
    weighting = spread / (sigmas * SIGMA_DATA) ** 2
    clean_f = clean.astype(jnp.float32)
    noisy = clean_f + sigmas * noise.astype(jnp.float32)
    x_own = (scale_in * noisy).astype(jnp.bfloat16)
    x_full = sent_to_all(x_own, MP).reshape(-1, x_own.shape[1])
    owned = snap_first.shape[0]
    stored = owned * lax.axis_size("cand")
    onehot = (snap_index[:, :, None] == jnp.arange(stored, dtype=jnp.int32)[None, None, :]).astype(
        jnp.float32
    )
    mixing = jnp.sum(blend[:, :, None] * onehot, 1)
    first_slot = lax.axis_index("cand") * owned
    other_mix = from_partner(mixing, "cand", 0)
    mix_rows = lax.dynamic_slice_in_dim(
        jnp.stack([mixing, other_mix], 0), first_slot, owned, 2
    )
    mix_mine, mix_give = mix_rows[0], mix_rows[1]
    taps, rows, width = snap_first.shape[1:]
    tokens = clean.shape[1]
    tall = taps * rows
    snap_first = snap_first.reshape(owned, tall, width)
    snap_second = snap_second.reshape(owned, tall, width)
    start = side * (tall - 128)
    got_second = from_partner(given_away(mix_give, snap_second, start, 8, 16), "cand", 0)
    got_first = from_partner(
        given_away(mix_give, snap_first, jnp.zeros((), jnp.int32), taps, rows), "cand", 0
    )
    turned = turned_second(mix_mine, snap_second, got_second, start, rows * tokens // 128)
    first_w = kept_first(mix_mine, snap_first, got_first, taps)
    sent = first_layer(first_w.reshape(2 * tall, width), x_full, turned)
    arrived = lax.all_to_all(
        sent.reshape(16, *sent.shape[2:]), (*ROWS, "dp"), split_axis=0, concat_axis=0, tiled=True
    ).reshape(sent.shape)
    shares = second_layer(arrived, rows, tokens).reshape(16, rows, tokens)
    shares = lax.all_to_all(shares, ("mp_2", "dp"), split_axis=0, concat_axis=0, tiled=True)
    features = shares.reshape(8, 2, rows, tokens).sum(axis=0)
    denoised_f = scale_skip[None, None, :] * noisy[None] + scale_out[None, None, :] * features
    partial_value = jnp.sum(
        weighting[None, None, :] * (denoised_f - clean_f[None]) ** 2, axis=(1, 2)
    )
    entries = clean.shape[0] * lax.axis_size(MP) * clean.shape[1] * lax.axis_size("dp")
    totals = over_copies(partial_value, (*MP, "dp"))
    losses = totals / entries
    return (losses, denoised_f.astype(jnp.bfloat16))


def solution(mesh):
    torus = Mesh(
        mesh.devices.reshape(mesh.shape["cand"], 4, 2, 8, mesh.shape["dp"]),
        ("cand", "mp_0", "mp_1", "mp_2", "dp"),
    )
    return jax.shard_map(
        on_device,
        mesh=torus,
        in_specs=(
            P(MP, "dp"),
            P(MP, "dp"),
            P("dp"),
            P("cand", None, MP, None),
            P("cand", None, MP, None),
            P("cand", None),
            P("cand", None),
        ),
        out_specs=(P("cand"), P("cand", MP, "dp")),
        check_vma=False,
    )
```

time: 285 us -> 126 us (0.44)
  other arithmetic: 141 us -> 2.9 us
  blocking collectives: 82.9 us -> 39.3 us
  Pallas kernels: 0 us -> 25.3 us
  waiting for transfers between devices: 29.1 us -> 35.3 us
  matrix products: 4.59 us -> 0 us
  starting transfers between devices: 21.5 us -> 17.9 us
    add x16 -> x0, other arithmetic: 92.1 us -> none  [accumulate(): totals[1] + coeff * second_snap[None]]
    all_to_all x1, blocking collectives: 58.4 us -> 22 us  [on_device(): lax.all_to_all(sent.reshape(16, *sent.shape[2:]), (*ROWS, 'dp'), split_ax...]
    mul x16 -> x0, other arithmetic: 25.7 us -> none  [accumulate(): coeff * second_snap[None]]
    pallas_call x0 -> x6, Pallas kernels: none -> 25.3 us  [the longest x2 8.98 us: given_away(): pl.pallas_call(give_kernel, out_shape=jax.ShapeDtypeStruct((members, chun...]
    unnamed x20 -> x0, other arithmetic: 15.5 us -> none
    all_to_all x1, waiting for transfers between devices: 0.01 us -> 12.6 us  [sent_to_all(): return lax.all_to_all(copies, axis, split_axis=0, concat_axis=0, tiled=True)]
    all_to_all x1, waiting for transfers between devices: 29.1 us -> 18.8 us  [on_device(): lax.all_to_all(shares, ('mp_2', 'dp'), split_axis=0, concat_axis=0, tiled...]
    all_to_all x2 -> x1, blocking collectives: 24.5 us -> 17.3 us  [sent_to_all(): return lax.all_to_all(copies, axis, split_axis=0, concat_axis=0, tiled=True)]
  transfers between devices with their start and end apart: 5 -> 5, of which waited for: 1 -> 4; matrix products, arithmetic and copies ran while one was open for 49% -> 2% of each run, Pallas kernels for 0% -> 11%
where the time goes in v2:
time: 126 us
  blocking collectives  39.3 us (31%)
  waiting for transfers between devices  35.3 us (28%)
  Pallas kernels  25.3 us (20%)
  starting transfers between devices  17.9 us (14%)
  local copies, waits for them, and re-layouts  4.15 us (3%)
  other arithmetic  2.9 us (2%)
    all_to_all x1, blocking collectives, on_device(): lax.all_to_all(sent.reshape(16, *sent.shape[2:]), (*ROWS, 'dp'), split_ax...  22 us
    all_to_all x1, waiting for transfers between devices, on_device(): lax.all_to_all(shares, ('mp_2', 'dp'), split_axis=0, concat_axis=0, tiled...  18.8 us
    all_to_all x1, blocking collectives, sent_to_all(): return lax.all_to_all(copies, axis, split_axis=0, concat_axis=0, tiled=True)  17.3 us
    all_to_all x1, starting transfers between devices, sent_to_all(): return lax.all_to_all(copies, axis, split_axis=0, concat_axis=0, tiled=True)  13 us
    all_to_all x1, waiting for transfers between devices, sent_to_all(): return lax.all_to_all(copies, axis, split_axis=0, concat_axis=0, tiled=True)  12.6 us
    pallas_call x2, Pallas kernels, given_away(): pl.pallas_call(give_kernel, out_shape=jax.ShapeDtypeStruct((members, chun...  8.98 us
    pallas_call x1, Pallas kernels, kept_first(): pl.pallas_call(keep_kernel, out_shape=jax.ShapeDtypeStruct((members, tall...  5.34 us
    all_to_all x1, starting transfers between devices, on_device(): lax.all_to_all(shares, ('mp_2', 'dp'), split_axis=0, concat_axis=0, tiled...  4.46 us
  transfers between devices with their start and end apart: 5, of which 4 were waited for; matrix products, arithmetic and copies ran while one was open for 2% of the time, Pallas kernels for 11%

profile of v2, /device:TPU:8, one launch (start us, length us, event | category | flops | bytes accessed | tf_op | source)
XLA Modules:
  0.0 125.7 jit_solution(11929484133012958765)
XLA Ops:
  0.6 0.8 select_reduce_fusion
  1.4 0.1 collective-permute-start
  1.5 0.7 add_exponential_fusion
  2.2 0.1 broadcast_in_dim.6
  2.3 0.1 reshape.77
  2.3 0.3 collective-permute-done
  2.7 0.1 dynamic-slice_maximum_fusion
  2.7 0.6 slice_bitcast_fusion
  3.3 5.0 %give.2 = f32[2,216,1536]{2,1,0:T(8,128)} custom-call(f32[2,8]{1,0:T(2,128)} %get-tuple-element.10.mix_ref, s32[1]{0:T(128)} %constant.37.clone.1.start_ref, bf16[8,216,1536]{2,1,0:T(8,128)(2,1)} %bitcast.15), custom_call_target="tpu_custom_call" | custom-call | flops 10616832 | bytes 7962624 | tf_op jit(solution)/shard_map/give/pallas_call | solution.py:84
  8.3 0.3 collective-permute-start.1
  8.6 0.0 copy-done.2
  8.6 0.0 copy-done.3
  8.6 1.1 broadcast_in_dim.7
  9.7 13.0 %all-to-all-start = ((bf16[64,24,384]{2,1,0:T(8,128)(2,1)}), bf16[64,24,384]{2,1,0:T(8,128)(2,1)S(1)}, u32[]{:S(2)}, u32[]{:S(2)}) async-start(bf16[64,24,384]{2,1,0:T(8,128)(2,1)} %broadcast_in_dim.7), calls=%async_computation | async-start | bytes 2359296 | tf_op jit(solution)/shard_map/all_to_all | solution.py:19
  22.8 4.0 %give.3 = f32[2,128,1536]{2,1,0:T(8,128)} custom-call(f32[2,8]{1,0:T(2,128)} %get-tuple-element.10.mix_ref, s32[1]{0:T(128)} %bitcast.7.start_ref, bf16[8,216,1536]{2,1,0:T(8,128)(2,1)} %bitcast.17), custom_call_target="tpu_custom_call" | custom-call | flops 6291456 | bytes 4718592 | tf_op jit(solution)/shard_map/give/pallas_call | solution.py:84
  26.8 0.1 collective-permute-start.2
  26.9 3.6 %collective-permute-done.2.got_ref = f32[2,128,1536]{2,1,0:T(8,128)S(1)} collective-permute-done((f32[2,128,1536]{2,1,0:T(8,128)}, f32[2,128,1536]{2,1,0:T(8,128)S(1)}, u32[]{:S(2)}, u32[]{:S(2)}) %collective-permute-start.2) | collective-permute-done | bytes 1572896 | tf_op jit(solution)/shard_map/ppermute | solution.py:23
  30.5 1.2 copy-done.1
  31.7 4.2 %turn.1.filled_ref = bf16[8,2,264,128]{3,2,1,0:T(8,128)(2,1)} custom-call(f32[2,8]{1,0:T(2,128)} %get-tuple-element.11.mix_ref, s32[1]{0:T(128)} %bitcast.7.start_ref, bf16[8,216,1536]{2,1,0:T(8,128)(2,1)} %bitcast.18, f32[2,128,1536]{2,1,0:T(8,128)} %copy-done.1), custom_call_target="tpu_custom_call" | custom-call | flops 6291456 | bytes 5505024 | tf_op jit(solution)/shard_map/turn/pallas_call | solution.py:224
  35.9 0.0 collective-permute-done.1.got_ref
  36.0 5.3 %keep.1 = bf16[2,216,1536]{2,1,0:T(8,128)(2,1)} custom-call(f32[2,8]{1,0:T(2,128)} %get-tuple-element.11.mix_ref, bf16[8,216,1536]{2,1,0:T(8,128)(2,1)} %bitcast.16, f32[2,216,1536]{2,1,0:T(8,128)} %collective-permute-done.1.got_ref), custom_call_target="tpu_custom_call" | custom-call | flops 10616832 | bytes 9289728 | tf_op jit(solution)/shard_map/keep/pallas_call | solution.py:148
  41.3 12.6 %all-to-all-done = bf16[64,24,384]{2,1,0:T(8,128)(2,1)S(1)} async-done(((bf16[64,24,384]{2,1,0:T(8,128)(2,1)}), bf16[64,24,384]{2,1,0:T(8,128)(2,1)S(1)}, u32[]{:S(2)}, u32[]{:S(2)}) %all-to-all-start) | async-done | bytes 1179680 | tf_op jit(solution)/shard_map/all_to_all | solution.py:19
  53.9 1.0 copy-done
  54.9 3.5 %first_layer.1 = bf16[8,2,264,128]{3,2,1,0:T(8,128)(2,1)} custom-call(bf16[432,1536]{1,0:T(8,128)(2,1)} %bitcast.20, bf16[1536,384]{1,0:T(8,128)(2,1)} %bitcast.21, bf16[8,2,264,128]{3,2,1,0:T(8,128)(2,1)} %turn.1.filled_ref), custom_call_target="tpu_custom_call", output_to_operand_aliasing={{}: (2, {})} | custom-call | flops 509607936 | bytes 2506752 | tf_op jit(solution)/shard_map/first_layer/pallas_call | solution.py:293
  58.4 22.0 %all_to_all.21 = bf16[16,264,128]{2,1,0:T(8,128)(2,1)} all-to-all(bf16[16,264,128]{2,1,0:T(8,128)(2,1)} %bitcast.19), channel_id=1, replica_groups=mesh['cand'=2,'mp_0'=4,'mp_1'=2,'mp_2'=8,'dp'=2] {'mp_0','mp_1','dp'}, dimensions={0} | all-to-all | bytes 2162688 | tf_op jit(solution)/shard_map/all_to_all | solution.py:392
  80.4 3.2 %second_layer.1 = f32[8,2,24,384]{3,2,1,0:T(8,128)} custom-call(bf16[8,2,264,128]{3,2,1,0:T(8,128)(2,1)} %bitcast.23), custom_call_target="tpu_custom_call" | custom-call | flops 603979776 | bytes 1671168 | tf_op jit(solution)/shard_map/second_layer/pallas_call | solution.py:340
  83.7 4.5 %all-to-all-start.2 = ((f32[16,24,384]{2,1,0:T(8,128)}), f32[16,24,384]{2,1,0:T(8,128)S(1)}, u32[]{:S(2)}, u32[]{:S(2)}) async-start(f32[16,24,384]{2,1,0:T(8,128)} %bitcast.24), calls=%async_computation.2 | async-start | bytes 1179648 | tf_op jit(solution)/shard_map/all_to_all | solution.py:396
  88.2 18.8 %all-to-all-done.2 = f32[16,24,384]{2,1,0:T(8,128)S(1)} async-done(((f32[16,24,384]{2,1,0:T(8,128)}), f32[16,24,384]{2,1,0:T(8,128)S(1)}, u32[]{:S(2)}, u32[]{:S(2)}) %all-to-all-start.2) | async-done | bytes 589856 | tf_op jit(solution)/shard_map/all_to_all | solution.py:396
  107.0 0.6 fusion
  107.7 17.3 %all_to_all.22 = f32[128,1,2]{2,1,0:T(1,128)S(1)} all-to-all(f32[128,1,2]{2,1,0:T(1,128)S(1)} %broadcast_in_dim.8), channel_id=1, replica_groups=mesh['cand'=2,'mp_0'=4,'mp_1'=2,'mp_2'=8,'dp'=2] {'mp_0','mp_1','mp_2','..., dimensions={0} | all-to-all | bytes 2048 | tf_op jit(solution)/shard_map/all_to_all | solution.py:19
  125.0 0.2 reduce_sum.39
  125.2 0.5 broadcast_multiply_fusion
  (9 shorter events, 0.1 us)
Async XLA Ops:
  1.4 1.2 collective-permute-start
  3.3 5.3 %copy-start.2 = (bf16[24,384]{1,0:T(8,128)(2,1)S(1)}, bf16[24,384]{1,0:T(8,128)(2,1)}, u32[]{:S(2)}) copy-start(bf16[24,384]{1,0:T(8,128)(2,1)} %param.7) | copy-start | bytes 55300
  3.3 5.3 %copy-start.3 = (bf16[24,384]{1,0:T(8,128)(2,1)S(1)}, bf16[24,384]{1,0:T(8,128)(2,1)}, u32[]{:S(2)}) copy-start(bf16[24,384]{1,0:T(8,128)(2,1)} %param.8) | copy-start | bytes 55300
  8.3 27.6 %collective-permute-start.1 = (f32[2,216,1536]{2,1,0:T(8,128)}, f32[2,216,1536]{2,1,0:T(8,128)}, u32[]{:S(2)}, u32[]{:S(2)}) collective-permute-start(f32[2,216,1536]{2,1,0:T(8,128)} %give.2), channel_id=1, source_target_pairs={{0,128},{128,0},{1,129},{129,1},{2,130},{130,2},{3,131},{131,3},{4... | collective-permute-start | bytes 7962632 | tf_op jit(solution)/shard_map/ppermute | solution.py:23
  9.7 44.1 %all-to-all-start = ((bf16[64,24,384]{2,1,0:T(8,128)(2,1)}), bf16[64,24,384]{2,1,0:T(8,128)(2,1)S(1)}, u32[]{:S(2)}, u32[]{:S(2)}) async-start(bf16[64,24,384]{2,1,0:T(8,128)(2,1)} %broadcast_in_dim.7), calls=%async_computation | async-start | bytes 2359296 | tf_op jit(solution)/shard_map/all_to_all | solution.py:19
  26.8 3.7 %collective-permute-start.2 = (f32[2,128,1536]{2,1,0:T(8,128)}, f32[2,128,1536]{2,1,0:T(8,128)S(1)}, u32[]{:S(2)}, u32[]{:S(2)}) collective-permute-start(f32[2,128,1536]{2,1,0:T(8,128)} %give.3), channel_id=1, source_target_pairs={{0,128},{128,0},{1,129},{129,1},{2,130},{130,2},{3,131},{131,3},{4... | collective-permute-start | bytes 4718600 | tf_op jit(solution)/shard_map/ppermute | solution.py:23
  30.5 1.2 copy-start.1
  53.9 1.0 copy-start
  83.7 23.3 %all-to-all-start.2 = ((f32[16,24,384]{2,1,0:T(8,128)}), f32[16,24,384]{2,1,0:T(8,128)S(1)}, u32[]{:S(2)}, u32[]{:S(2)}) async-start(f32[16,24,384]{2,1,0:T(8,128)} %bitcast.24), calls=%async_computation.2 | async-start | bytes 1179648 | tf_op jit(solution)/shard_map/all_to_all | solution.py:396

commit v3 on v2

v3 whole, which is shorter than its diff:
```python
import jax
import jax.numpy as jnp
from jax import lax
from jax.experimental import pallas as pl
from jax.experimental.pallas import tpu as pltpu
from jax.sharding import Mesh
from jax.sharding import PartitionSpec as P


LEVELS = 32
MP = ("mp_0", "mp_1", "mp_2")
ROWS = ("mp_0", "mp_1")


SIGMA_DATA = 0.5


def from_partner(value, axis, apart):
    return lax.ppermute(value, axis, [(i, i ^ 1 << apart) for i in range(lax.axis_size(axis))])


ANY = pl.BlockSpec(memory_space=pl.ANY)
SCALARS = pl.BlockSpec(memory_space=pltpu.SMEM)
WHOLE = pl.BlockSpec(memory_space=pltpu.VMEM)
MIB = 1024 * 1024
SMALL = pltpu.CompilerParams(vmem_limit_bytes=8 * MIB)


def OUT(shape, dtype):
    return pltpu.VMEM(shape, dtype)


def FAR(value):
    return pltpu.with_memory_space_constraint(value, pltpu.HBM)


def IN(value):
    return pltpu.with_memory_space_constraint(value, pltpu.VMEM)


def token_scales(level_ref, shape):
    image = lax.broadcasted_iota(jnp.int32, shape, 1) >> 6
    level = jnp.zeros(shape, jnp.float32)
    for i in range(level_ref.shape[0]):
        level = jnp.where(image == i, level_ref[i].astype(jnp.float32), level)
    ratio = 2.0 * level / (LEVELS - 1) - 1.0
    sigmas = jnp.exp(-0.4 + 2.0 * ratio)
    spread = sigmas * sigmas + SIGMA_DATA * SIGMA_DATA
    return sigmas, spread


def prepare_kernel(level_ref, clean_ref, noise_ref, out_ref):
    sigmas, spread = token_scales(level_ref, clean_ref.shape)
    noisy = clean_ref[...].astype(jnp.float32) + sigmas * noise_ref[...].astype(jnp.float32)
    value = (1.0 / jnp.sqrt(spread) * noisy).astype(jnp.bfloat16)
    for p in range(out_ref.shape[0]):
        out_ref[p] = value


def prepared(level_index, clean, noise, copies):
    rows, tokens = clean.shape
    return pl.pallas_call(
        prepare_kernel,
        out_shape=OUT((copies, rows, tokens), jnp.bfloat16),
        in_specs=[SCALARS, WHOLE, WHOLE],
        out_specs=WHOLE,
        compiler_params=SMALL,
        cost_estimate=pl.CostEstimate(
            flops=20 * rows * tokens,
            bytes_accessed=2 * (copies + 2) * rows * tokens,
            transcendentals=3 * rows * tokens,
        ),
        name="prepare",
    )(level_index, FAR(clean), FAR(noise))


def final_kernel(level_ref, clean_ref, noise_ref, share_ref, out_ref, loss_ref):
    sigmas, spread = token_scales(level_ref, clean_ref.shape)
    clean = clean_ref[...].astype(jnp.float32)
    noisy = clean + sigmas * noise_ref[...].astype(jnp.float32)
    scale_skip = SIGMA_DATA * SIGMA_DATA / spread
    scale_out = sigmas * SIGMA_DATA / jnp.sqrt(spread)
    weighting = spread / ((sigmas * SIGMA_DATA) * (sigmas * SIGMA_DATA))
    lane = lax.broadcasted_iota(jnp.int32, loss_ref.shape, 2)
    losses = jnp.zeros(loss_ref.shape, jnp.float32)
    for c in range(out_ref.shape[0]):
        feature = share_ref[0, c]
        for z in range(1, share_ref.shape[0]):
            feature = feature + share_ref[z, c]
        denoised = scale_skip * noisy + scale_out * feature
        out_ref[c] = denoised.astype(jnp.bfloat16)
        away = denoised - clean
        losses = jnp.where(lane == c, jnp.sum(weighting * (away * away)), losses)
    loss_ref[...] = losses


def finished(level_index, clean, noise, shares, copies):
    rows, tokens = clean.shape
    members = shares.shape[1]
    return pl.pallas_call(
        final_kernel,
        out_shape=(
            jax.ShapeDtypeStruct((members, rows, tokens), jnp.bfloat16),
            OUT((copies, 1, 128), jnp.float32),
        ),
        in_specs=[SCALARS, WHOLE, WHOLE, WHOLE],
        out_specs=(WHOLE, WHOLE),
        compiler_params=SMALL,
        cost_estimate=pl.CostEstimate(
            flops=40 * members * rows * tokens,
            bytes_accessed=4 * shares.size + 8 * rows * tokens,
            transcendentals=3 * rows * tokens,
        ),
        name="final",
    )(level_index, clean, noise, IN(shares))


def weighted_rows(mix_ref, row, values):
    total = None
    for n, value in enumerate(values):
        term = mix_ref[row, n] * value
        total = term if total is None else total + term
    return total


def give_kernel(mix_ref, start_ref, snap_ref, out_ref):
    snaps = snap_ref.shape[0]
    members, tall, width = out_ref.shape
    rows, step = 8, 768
    start = start_ref[0]

    @pl.loop(0, tall // rows)
    def _(k):
        source = pl.ds(pl.multiple_of(start + k * rows, 8), rows)
        target = pl.ds(pl.multiple_of(k * rows, 8), rows)
        for j in range(width // step):
            cols = slice(j * step, (j + 1) * step)
            values = [snap_ref[n, source, cols].astype(jnp.float32) for n in range(snaps)]
            for row in range(members):
                out_ref[row, target, cols] = weighted_rows(mix_ref, row, values)


def given_away(mix, snap, start, tall):
    snaps, _, width = snap.shape
    members = mix.shape[0]
    return pl.pallas_call(
        give_kernel,
        out_shape=OUT((members, tall, width), jnp.float32),
        in_specs=[SCALARS, SCALARS, WHOLE],
        out_specs=WHOLE,
        cost_estimate=pl.CostEstimate(
            flops=2 * members * tall * width * snaps,
            bytes_accessed=(2 * snaps + 4 * members) * tall * width,
            transcendentals=0,
        ),
        compiler_params=SMALL,
        name="give",
    )(mix, start.reshape(1), IN(snap))


def keep_kernel(mix_ref, snap_ref, got_ref, out_ref):
    snaps = snap_ref.shape[0]
    members, tall, width = out_ref.shape
    rows, step = 8, 768

    @pl.loop(0, tall // rows)
    def _(k):
        span = pl.ds(pl.multiple_of(k * rows, 8), rows)
        for j in range(width // step):
            cols = slice(j * step, (j + 1) * step)
            values = [snap_ref[n, span, cols].astype(jnp.float32) for n in range(snaps)]
            for row in range(members):
                total = weighted_rows(mix_ref, row, values) + got_ref[row, span, cols]
                out_ref[row, span, cols] = total.astype(jnp.bfloat16)


def kept_first(mix, snap, got):
    snaps, tall, width = snap.shape
    members = mix.shape[0]
    return pl.pallas_call(
        keep_kernel,
        out_shape=OUT((members, tall, width), jnp.bfloat16),
        in_specs=[SCALARS, WHOLE, WHOLE],
        out_specs=WHOLE,
        cost_estimate=pl.CostEstimate(
            flops=2 * members * tall * width * snaps,
            bytes_accessed=(2 * snaps + 6 * members) * tall * width,
            transcendentals=0,
        ),
        compiler_params=SMALL,
        name="keep",
    )(mix, IN(snap), IN(got))


def turn_kernel(mix_ref, start_ref, snap_ref, got_ref, out_ref):
    snaps = snap_ref.shape[0]
    members, rows, width = got_ref.shape
    owners = out_ref.shape[0]
    each = width // owners
    source = pl.ds(pl.multiple_of(start_ref[0], 8), rows)

    @pl.loop(0, owners // 2)
    def _(k):
        for part in range(2 * each // 128):
            low = part * 128
            cols = pl.ds(pl.multiple_of(k * 2 * each + low, 128), 128)
            values = [snap_ref[n, source, cols].astype(jnp.float32) for n in range(snaps)]
            for row in range(members):
                total = weighted_rows(mix_ref, row, values) + got_ref[row, :, cols]
                turn = total.T.astype(jnp.bfloat16)
                for owner in range(2):
                    first, last = max(low, owner * each), min(low + 128, (owner + 1) * each)
                    if first < last:
                        span = slice(first - owner * each, last - owner * each)
                        out_ref[2 * k + owner, row, span, :] = turn[first - low : last - low]


def turned_second(mix, snap, got, start, extra):
    snaps, _, width = snap.shape
    members, rows, _ = got.shape
    owners = 8
    return pl.pallas_call(
        turn_kernel,
        out_shape=OUT((owners, members, width // owners + extra, rows), jnp.bfloat16),
        in_specs=[SCALARS, SCALARS, WHOLE, WHOLE],
        out_specs=WHOLE,
        cost_estimate=pl.CostEstimate(
            flops=2 * members * rows * width * snaps,
            bytes_accessed=(2 * snaps + 6 * members) * rows * width,
            transcendentals=0,
        ),
        compiler_params=SMALL,
        name="turn",
    )(mix, start.reshape(1), IN(snap), IN(got))


TAPS = [(a, b) for a in (-1, 0, 1) for b in (-1, 0, 1)]


def shifted(values, down_by, right_by):
    tokens = values.shape[1]
    offset = down_by * 8 + right_by
    moved = values if offset == 0 else pltpu.roll(values, (-offset) % tokens, 1)
    token = lax.broadcasted_iota(jnp.int32, values.shape, 1)
    row = ((token >> 3) & 7) + down_by
    col = (token & 7) + right_by
    inside = (row >= 0) & (row < 8) & (col >= 0) & (col < 8)
    return jnp.where(inside, moved, 0.0)


def first_kernel(w_ref, x_ref, filled_ref, out_ref, acc_ref):
    acc_ref[...] = jnp.dot(w_ref[...], x_ref[...], preferred_element_type=jnp.float32)
    owners, members, end, lanes = out_ref.shape
    rows = acc_ref.shape[0] // (members * len(TAPS))
    tokens = acc_ref.shape[1]
    for c in range(members):
        total = None
        for k, (a, b) in enumerate(TAPS):
            start = (c * len(TAPS) + k) * rows
            term = shifted(acc_ref[start : start + rows, :], a, b)
            total = term if total is None else total + term
        total = total * (1.0 / (1.0 + jnp.exp(-total)))
        parts = [total[:, j * lanes : (j + 1) * lanes] for j in range(tokens // lanes)]
        hidden = jnp.concatenate(parts, 0).astype(jnp.bfloat16)
        for g in range(owners):
            out_ref[g, c, end - hidden.shape[0] :, :] = hidden


def first_layer(w, x, filled):
    tall, width = w.shape
    tokens = x.shape[1]
    return pl.pallas_call(
        first_kernel,
        out_shape=OUT(filled.shape, filled.dtype),
        in_specs=[WHOLE, WHOLE, WHOLE],
        out_specs=WHOLE,
        input_output_aliases={2: 0},
        scratch_shapes=[pltpu.VMEM((tall, tokens), jnp.float32)],
        cost_estimate=pl.CostEstimate(
            flops=2 * tall * width * tokens,
            bytes_accessed=2 * tall * width + 2 * width * tokens,
            transcendentals=tall * tokens // len(TAPS),
        ),
        compiler_params=SMALL,
        name="first_layer",
    )(IN(w), IN(x), IN(filled))


def second_kernel(got_ref, out_ref, acc_ref):
    sources, halves, _, lanes = got_ref.shape
    owners, _, rows, tokens = out_ref.shape
    each = owners * rows
    cut = lanes
    blank = jnp.zeros((halves * lanes - len(TAPS) * rows, tokens), jnp.float32)
    for half in range(halves):
        total = None
        for s in range(sources):
            parts = [
                got_ref[s, half, each + j * rows : each + (j + 1) * rows, :].astype(jnp.float32)
                for j in range(tokens // lanes)
            ]
            h = jnp.concatenate(parts, 1)
            stack = jnp.concatenate([shifted(h, a, b) for a, b in TAPS], 0)
            stack = jnp.concatenate([stack[:cut], blank, stack[cut:]], 0).astype(jnp.bfloat16)
            w = jnp.concatenate([got_ref[s, 0, :each, :], got_ref[s, 1, :each, :]], 1)
            term = jnp.dot(w, stack, preferred_element_type=jnp.float32)
            total = term if total is None else total + term
        acc_ref[...] = total
        for z in range(owners):
            out_ref[z, half] = acc_ref[z * rows : (z + 1) * rows, :]


def second_layer(got, rows, tokens):
    sources, halves, _, _ = got.shape
    return pl.pallas_call(
        second_kernel,
        out_shape=OUT((8, halves, rows, tokens), jnp.float32),
        in_specs=[WHOLE],
        out_specs=WHOLE,
        scratch_shapes=[pltpu.VMEM((8 * rows, tokens), jnp.float32)],
        cost_estimate=pl.CostEstimate(
            flops=2 * sources * 8 * rows * 256 * 2 * tokens,
            bytes_accessed=2 * got.size + 4 * 16 * rows * tokens,
            transcendentals=0,
        ),
        compiler_params=SMALL,
        name="second_layer",
    )(IN(got))


def mix_of(blend, snap_index, first, count):
    stored = first + jnp.arange(count, dtype=jnp.int32)
    chosen = (snap_index[:, :, None] == stored[None, None, :]).astype(jnp.float32)
    return jnp.sum(blend[:, :, None] * chosen, 1)


def computed(clean, noise, level_index, snap_first, snap_second, blend, snap_index):
    side = lax.axis_index("dp").astype(jnp.int32)
    owned, taps, rows, width = snap_first.shape
    tokens = clean.shape[1]
    tall = taps * rows
    snap_first = snap_first.reshape(owned, tall, width)
    snap_second = snap_second.reshape(owned, tall, width)
    start = side * (tall - 128)
    group = lax.axis_index("cand")
    mix_mine = mix_of(blend, snap_index, group * owned, owned)
    mix_give = from_partner(mix_of(blend, snap_index, (1 - group) * owned, owned), "cand", 0)
    copies = prepared(level_index, clean, noise, lax.axis_size("mp_2"))
    x_line = lax.all_to_all(copies, "mp_2", split_axis=0, concat_axis=0, tiled=True)
    x_line = x_line.reshape(-1, tokens)
    x_line = jnp.broadcast_to(x_line, (lax.axis_size(ROWS), *x_line.shape))
    x_full = lax.all_to_all(x_line, ROWS, split_axis=0, concat_axis=0, tiled=True)
    x_full = x_full.reshape(-1, tokens)
    give_second = given_away(mix_give, snap_second, start, 128)
    got_second = from_partner(give_second, "cand", 0)
    mix_give, _ = lax.optimization_barrier((mix_give, give_second))
    give_first = given_away(mix_give, snap_first, jnp.zeros((), jnp.int32), tall)
    got_first = from_partner(give_first, "cand", 0)
    mix_mine, _ = lax.optimization_barrier((mix_mine, give_first))
    turned = turned_second(mix_mine, snap_second, got_second, start, rows * tokens // 128)
    mix_mine, turned = lax.optimization_barrier((mix_mine, turned))
    first_w = kept_first(mix_mine, snap_first, got_first)
    sent = first_layer(first_w.reshape(2 * tall, width), x_full, turned)
    arrived = lax.all_to_all(
        sent.reshape(16, *sent.shape[2:]), (*ROWS, "dp"), split_axis=0, concat_axis=0, tiled=True
    ).reshape(sent.shape)
    shares = second_layer(arrived, rows, tokens).reshape(16, rows, tokens)
    shares = lax.all_to_all(shares, ("mp_2", "dp"), split_axis=0, concat_axis=0, tiled=True)
    shares = shares.reshape(8, 2, rows, tokens)
    everyone = (*MP, "dp")
    denoised, partial = finished(level_index, clean, noise, shares, lax.axis_size(everyone))
    partial = lax.all_to_all(partial, everyone, split_axis=0, concat_axis=0, tiled=True)
    entries = clean.shape[0] * lax.axis_size(MP) * tokens * lax.axis_size("dp")
    losses = jnp.sum(partial, axis=(0, 1))[: denoised.shape[0]] / entries
    return (losses, denoised)


def solution(mesh):
    torus = Mesh(
        mesh.devices.reshape(mesh.shape["cand"], 4, 2, 8, mesh.shape["dp"]),
        ("cand", "mp_0", "mp_1", "mp_2", "dp"),
    )
    return jax.shard_map(
        computed,
        mesh=torus,
        in_specs=(
            P(MP, "dp"),
            P(MP, "dp"),
            P("dp"),
            P("cand", None, MP, None),
            P("cand", None, MP, None),
            P("cand", None),
            P("cand", None),
        ),
        out_specs=(P("cand"), P("cand", MP, "dp")),
        check_vma=False,
    )
```

time: 126 us -> 120 us (0.952)
  blocking collectives: 39.3 us -> 80.3 us
  waiting for transfers between devices: 35.3 us -> 5.27 us
  starting transfers between devices: 17.9 us -> 6.57 us
  Pallas kernels: 25.3 us -> 18.5 us
  local copies, waits for them, and re-layouts: 4.15 us -> 7.05 us
  other arithmetic: 2.9 us -> 1.46 us
    all_to_all x2 -> x4, blocking collectives: 39.3 us -> 80.3 us  [the longest x1 23.5 us: computed(): lax.all_to_all(shares, ('mp_2', 'dp'), split_axis=0, concat_axis=0, tiled...]
    all_to_all x2 -> x1, waiting for transfers between devices: 31.4 us -> 4.12 us  [computed(): lax.all_to_all(x_line, ROWS, split_axis=0, concat_axis=0, tiled=True)]
    all_to_all x2 -> x1, starting transfers between devices: 17.5 us -> 5.97 us  [computed(): lax.all_to_all(x_line, ROWS, split_axis=0, concat_axis=0, tiled=True)]
    pallas_call x6 -> x8, Pallas kernels: 25.3 us -> 18.5 us  [the longest x2 6.08 us: given_away(): pl.pallas_call(give_kernel, out_shape=OUT((members, tall, width), jnp.flo...]
    unnamed x8 -> x16, local copies, waits for them, and re-layouts: 2.24 us -> 5.84 us
    ppermute x3, waiting for transfers between devices: 3.93 us -> 1.15 us  [from_partner(): lax.ppermute(value, axis, [(i, i ^ 1 << apart) for i in range(lax.axis_si...]
  transfers between devices with their start and end apart: 5 -> 4, of which waited for: 4 -> 2; matrix products, arithmetic and copies ran while one was open for 2% -> 1% of each run, Pallas kernels for 11% -> 7%
where the time goes in v3:
time: 120 us
  blocking collectives  80.3 us (67%)
  Pallas kernels  18.5 us (15%)
  local copies, waits for them, and re-layouts  7.05 us (6%)
  starting transfers between devices  6.57 us (5%)
  waiting for transfers between devices  5.27 us (4%)
  other arithmetic  1.46 us (1%)
    all_to_all x1, blocking collectives, computed(): lax.all_to_all(shares, ('mp_2', 'dp'), split_axis=0, concat_axis=0, tiled...  23.5 us
    all_to_all x1, blocking collectives, computed(): lax.all_to_all(sent.reshape(16, *sent.shape[2:]), (*ROWS, 'dp'), split_ax...  21.5 us
    all_to_all x1, blocking collectives, computed(): lax.all_to_all(copies, 'mp_2', split_axis=0, concat_axis=0, tiled=True)  18 us
    all_to_all x1, blocking collectives, computed(): lax.all_to_all(partial, everyone, split_axis=0, concat_axis=0, tiled=True)  17.3 us
    pallas_call x2, Pallas kernels, given_away(): pl.pallas_call(give_kernel, out_shape=OUT((members, tall, width), jnp.flo...  6.08 us
    all_to_all x1, starting transfers between devices, computed(): lax.all_to_all(x_line, ROWS, split_axis=0, concat_axis=0, tiled=True)  5.97 us
    unnamed x16, local copies, waits for them, and re-layouts  5.84 us
    all_to_all x1, waiting for transfers between devices, computed(): lax.all_to_all(x_line, ROWS, split_axis=0, concat_axis=0, tiled=True)  4.12 us
  transfers between devices with their start and end apart: 4, of which 2 were waited for; matrix products, arithmetic and copies ran while one was open for 1% of the time, Pallas kernels for 7%

profile of v3, /device:TPU:8, one launch (start us, length us, event | category | flops | bytes accessed | tf_op | source)
XLA Modules:
  0.0 119.9 jit_solution(6046017065688584529)
XLA Ops:
  0.6 0.8 select_reduce_fusion
  1.4 0.1 collective-permute-start
  1.5 1.1 collective-permute-done.mix_ref
  2.7 2.5 %copy-done.1 = bf16[8,9,24,1536]{3,2,1,0:T(8,128)(2,1)S(1)} copy-done((bf16[8,9,24,1536]{3,2,1,0:T(8,128)(2,1)S(1)}, bf16[8,9,24,1536]{3,2,1,0:T(8,128)(2,1)}, u32[]{:S(2)}) %copy-start.1) | copy-done | bytes 5308440
  5.2 1.8 %give.2 = f32[2,128,1536]{2,1,0:T(8,128)S(1)} custom-call(f32[2,8]{1,0:T(2,128)S(1)} %collective-permute-done.mix_ref, s32[1]{0:T(128)} %bitcast.start_ref, bf16[8,216,1536]{2,1,0:T(8,128)(2,1)S(1)} %bitcast.14), custom_call_target="tpu_custom_call" | custom-call | flops 6291456 | bytes 4718592 | tf_op jit(solution)/shard_map/give/pallas_call | solution.py:146
  7.0 0.7 copy-done
  7.7 4.3 %give.3 = f32[2,216,1536]{2,1,0:T(8,128)} custom-call(f32[2,8]{1,0:T(2,128)S(1)} %collective-permute-done.mix_ref, s32[1]{0:T(128)} %constant.21.clone.1.start_ref, bf16[8,216,1536]{2,1,0:T(8,128)(2,1)S(1)} %bitcast.10), custom_call_target="tpu_custom_call" | custom-call | flops 10616832 | bytes 7962624 | tf_op jit(solution)/shard_map/give/pallas_call | solution.py:146
  11.9 0.2 collective-permute-start.2
  12.1 0.3 collective-permute-start.1
  12.5 0.0 copy-done.5
  12.5 0.8 prepare.1
  13.3 18.0 %all_to_all.25 = bf16[8,24,384]{2,1,0:T(8,128)(2,1)S(1)} all-to-all(bf16[8,24,384]{2,1,0:T(8,128)(2,1)S(1)} %prepare.1), channel_id=1, replica_groups=mesh['cand'=2,'mp_0'=4,'mp_1'=2,'mp_2'=8,'dp'=2] {'mp_2'}, dimensions={0} | all-to-all | bytes 294912 | tf_op jit(solution)/shard_map/all_to_all | solution.py:349
  31.3 1.2 %broadcast_in_dim.2 = bf16[8,192,384]{2,1,0:T(8,128)(2,1)} broadcast(bf16[192,384]{1,0:T(8,128)(2,1)S(1)} %bitcast.21), dimensions={1,2} | broadcast | bytes 1327104 | tf_op jit(solution)/shard_map/broadcast_in_dim | solution.py:351
  32.5 6.0 %all-to-all-start.1 = ((bf16[8,192,384]{2,1,0:T(8,128)(2,1)}), bf16[8,192,384]{2,1,0:T(8,128)(2,1)}, u32[]{:S(2)}, u32[]{:S(2)}) async-start(bf16[8,192,384]{2,1,0:T(8,128)(2,1)} %broadcast_in_dim.2), calls=%async_computation.1 | async-start | bytes 2359296 | tf_op jit(solution)/shard_map/all_to_all | solution.py:352
  38.5 0.0 collective-permute-done.1.got_ref
  38.5 0.0 copy-start.2
  38.5 2.6 %copy-done.2 = bf16[8,9,24,1536]{3,2,1,0:T(8,128)(2,1)S(1)} copy-done((bf16[8,9,24,1536]{3,2,1,0:T(8,128)(2,1)S(1)}, bf16[8,9,24,1536]{3,2,1,0:T(8,128)(2,1)}, u32[]{:S(2)}) %copy-start.2) | copy-done | bytes 5308440
  41.1 2.9 %turn.1.filled_ref = bf16[8,2,264,128]{3,2,1,0:T(8,128)(2,1)S(1)} custom-call(f32[2,8]{1,0:T(2,128)S(1)} %get-tuple-element.10.mix_ref, s32[1]{0:T(128)} %bitcast.start_ref, bf16[8,216,1536]{2,1,0:T(8,128)(2,1)S(1)} %bitcast.15, f32[2,128,1536]{2,1,0:T(8,128)} %collective-permute-done.1.got_ref), custom_call_target="tpu_custom_call" | custom-call | flops 6291456 | bytes 5505024 | tf_op jit(solution)/shard_map/turn/pallas_call | solution.py:222
  44.1 0.0 collective-permute-done.2.got_ref
  44.1 0.0 slice-done
  44.1 0.0 slice-done.1
  44.1 4.1 %keep.1 = bf16[2,216,1536]{2,1,0:T(8,128)(2,1)S(1)} custom-call(f32[2,8]{1,0:T(2,128)S(1)} %get-tuple-element.10.mix_ref, bf16[8,216,1536]{2,1,0:T(8,128)(2,1)S(1)} %bitcast.13, f32[2,216,1536]{2,1,0:T(8,128)} %collective-permute-done.2.got_ref), custom_call_target="tpu_custom_call" | custom-call | flops 10616832 | bytes 9289728 | tf_op jit(solution)/shard_map/keep/pallas_call | solution.py:180
  48.2 4.1 %all-to-all-done.1 = bf16[8,192,384]{2,1,0:T(8,128)(2,1)} async-done(((bf16[8,192,384]{2,1,0:T(8,128)(2,1)}), bf16[8,192,384]{2,1,0:T(8,128)(2,1)}, u32[]{:S(2)}, u32[]{:S(2)}) %all-to-all-start.1) | async-done | bytes 1179680 | tf_op jit(solution)/shard_map/all_to_all | solution.py:352
  52.3 2.3 %first_layer.1 = bf16[8,2,264,128]{3,2,1,0:T(8,128)(2,1)S(1)} custom-call(bf16[432,1536]{1,0:T(8,128)(2,1)S(1)} %bitcast.17, bf16[1536,384]{1,0:T(8,128)(2,1)} %bitcast.5.x_ref, bf16[8,2,264,128]{3,2,1,0:T(8,128)(2,1)S(1)} %turn.1.filled_ref), custom_call_target="tpu_custom_call", output_to_operand_aliasing={{}: (2, {})} | custom-call | flops 509607936 | bytes 2506752 | tf_op jit(solution)/shard_map/first_layer/pallas_call | solution.py:272
  54.6 21.5 %all_to_all.26 = bf16[16,264,128]{2,1,0:T(8,128)(2,1)S(1)} all-to-all(bf16[16,264,128]{2,1,0:T(8,128)(2,1)S(1)} %bitcast.16), channel_id=1, replica_groups=mesh['cand'=2,'mp_0'=4,'mp_1'=2,'mp_2'=8,'dp'=2] {'mp_0','mp_1','dp'}, dimensions={0} | all-to-all | bytes 2162688 | tf_op jit(solution)/shard_map/all_to_all | solution.py:364
  76.0 1.2 second_layer.1
  77.2 23.5 %all_to_all.27 = f32[16,24,384]{2,1,0:T(8,128)S(1)} all-to-all(f32[16,24,384]{2,1,0:T(8,128)S(1)} %bitcast.20), channel_id=1, replica_groups=mesh['cand'=2,'mp_0'=4,'mp_1'=2,'mp_2'=8,'dp'=2] {'mp_2','dp'}, dimensions={0} | all-to-all | bytes 1179648 | tf_op jit(solution)/shard_map/all_to_all | solution.py:368
  100.7 0.0 copy-done.4
  100.7 1.2 %final.1 = (bf16[2,24,384]{2,1,0:T(8,128)(2,1)}, f32[128,1,128]{2,1,0:T(1,128)S(1)}) custom-call(s32[6]{0:T(128)S(1)} %copy-done.5, bf16[24,384]{1,0:T(8,128)(2,1)S(1)} %copy-done.3, bf16[24,384]{1,0:T(8,128)(2,1)S(1)} %copy-done.4, f32[8,2,24,384]{3,2,1,0:T(8,128)S(1)} %bitcast.18), custom_call_target="tpu_custom_call" | custom-call | flops 737280 | bytes 663552 | tf_op jit(solution)/shard_map/final/pallas_call | solution.py:100
  101.9 17.3 %all_to_all.28 = f32[128,1,128]{2,1,0:T(1,128)S(1)} all-to-all(f32[128,1,128]{2,1,0:T(1,128)S(1)} %get-tuple-element.12), channel_id=1, replica_groups=mesh['cand'=2,'mp_0'=4,'mp_1'=2,'mp_2'=8,'dp'=2] {'mp_0','mp_1','mp_2','..., dimensions={0} | all-to-all | bytes 131072 | tf_op jit(solution)/shard_map/all_to_all | solution.py:372
  119.2 0.2 reduce_sum.29
  119.4 0.5 slice_multiply_fusion
  (10 shorter events, 0.0 us)
Async XLA Ops:
  1.4 1.2 %collective-permute-start = (f32[2,8]{1,0:T(2,128)S(1)}, f32[2,8]{1,0:T(2,128)S(1)}, u32[]{:S(2)}, u32[]{:S(2)}) collective-permute-start(f32[2,8]{1,0:T(2,128)S(1)} %get-tuple-element.14), channel_id=1, source_target_pairs={{0,128},{128,0},{1,129},{129,1},{2,130},{130,2},{3,131},{131,3},{4... | collective-permute-start | bytes 200 | tf_op jit(solution)/shard_map/ppermute | solution.py:19
  2.7 2.5 %copy-start.1 = (bf16[8,9,24,1536]{3,2,1,0:T(8,128)(2,1)S(1)}, bf16[8,9,24,1536]{3,2,1,0:T(8,128)(2,1)}, u32[]{:S(2)}) copy-start(bf16[8,9,24,1536]{3,2,1,0:T(8,128)(2,1)} %param.11) | copy-start | bytes 15925252
  5.2 2.5 %copy-start = (bf16[8,9,24,1536]{3,2,1,0:T(8,128)(2,1)S(1)}, bf16[8,9,24,1536]{3,2,1,0:T(8,128)(2,1)}, u32[]{:S(2)}) copy-start(bf16[8,9,24,1536]{3,2,1,0:T(8,128)(2,1)} %param.10) | copy-start | bytes 15925252
  7.7 4.8 %copy-start.5 = (s32[6]{0:T(128)S(1)}, s32[6]{0:T(128)}, u32[]{:S(2)}) copy-start(s32[6]{0:T(128)} %level_ref.3) | copy-start | bytes 76
  11.9 32.1 %collective-permute-start.2 = (f32[2,216,1536]{2,1,0:T(8,128)}, f32[2,216,1536]{2,1,0:T(8,128)}, u32[]{:S(2)}, u32[]{:S(2)}) collective-permute-start(f32[2,216,1536]{2,1,0:T(8,128)} %give.3), channel_id=1, source_target_pairs={{0,128},{128,0},{1,129},{129,1},{2,130},{130,2},{3,131},{131,3},{4... | collective-permute-start | bytes 7962632 | tf_op jit(solution)/shard_map/ppermute | solution.py:19
  12.1 26.4 %collective-permute-start.1 = (f32[2,128,1536]{2,1,0:T(8,128)S(1)}, f32[2,128,1536]{2,1,0:T(8,128)}, u32[]{:S(2)}, u32[]{:S(2)}) collective-permute-start(f32[2,128,1536]{2,1,0:T(8,128)S(1)} %give.2), channel_id=1, source_target_pairs={{0,128},{128,0},{1,129},{129,1},{2,130},{130,2},{3,131},{131,3},{4... | collective-permute-start | bytes 4718600 | tf_op jit(solution)/shard_map/ppermute | solution.py:19
  32.5 11.6 %slice-start = ((s8[5308416]{0:T(1024)(128)(4,1)}), s8[1114112]{0:T(1024)(128)(4,1)S(1)}, s32[]{:S(2)}) async-start(s8[5308416]{0:T(1024)(128)(4,1)} %bitcast.11), calls=%async_computation.5 | async-start | bytes 2228224
  32.5 19.8 %all-to-all-start.1 = ((bf16[8,192,384]{2,1,0:T(8,128)(2,1)}), bf16[8,192,384]{2,1,0:T(8,128)(2,1)}, u32[]{:S(2)}, u32[]{:S(2)}) async-start(bf16[8,192,384]{2,1,0:T(8,128)(2,1)} %broadcast_in_dim.2), calls=%async_computation.1 | async-start | bytes 2359296 | tf_op jit(solution)/shard_map/all_to_all | solution.py:352
  38.5 5.6 %slice-start.1 = ((s8[5308416]{0:T(1024)(128)(4,1)}), s8[4194304]{0:T(1024)(128)(4,1)S(1)}, s32[]{:S(2)}) async-start(s8[5308416]{0:T(1024)(128)(4,1)} %bitcast.11), calls=%async_computation.6 | async-start | bytes 8388608
  38.5 2.7 %copy-start.2 = (bf16[8,9,24,1536]{3,2,1,0:T(8,128)(2,1)S(1)}, bf16[8,9,24,1536]{3,2,1,0:T(8,128)(2,1)}, u32[]{:S(2)}) copy-start(bf16[8,9,24,1536]{3,2,1,0:T(8,128)(2,1)} %param.11) | copy-start | bytes 15925252
  76.0 24.7 %copy-start.3 = (bf16[24,384]{1,0:T(8,128)(2,1)S(1)}, bf16[24,384]{1,0:T(8,128)(2,1)}, u32[]{:S(2)}) copy-start(bf16[24,384]{1,0:T(8,128)(2,1)} %clean_ref.3) | copy-start | bytes 55300
  76.0 24.7 %copy-start.4 = (bf16[24,384]{1,0:T(8,128)(2,1)S(1)}, bf16[24,384]{1,0:T(8,128)(2,1)}, u32[]{:S(2)}) copy-start(bf16[24,384]{1,0:T(8,128)(2,1)} %noise_ref.3) | copy-start | bytes 55300
